TPU v7x, 512 devices: a whole 4x4x16 slice. The times are simulated.
512 devices in a mesh: owner: 64 (over z_hi, y, core), rows: 8 (over z_lo, x).
Axes of the slice: x: 4, y: 4, z: 16 (z_hi: 8, z_lo: 2; z = z_hi * 2 + z_lo), core: 2. Of those that a mesh axis runs over, the one named last changes fastest.
Arguments:
- w_gate: float32 [64, 2048, 1024], P('owner', 'rows'), may hold values from -0.1875 to 0.1875
- avg_gate: float32 [64, 2048, 1024], P('owner', 'rows'), may hold values from -0.125 to 0.125
- w_up: float32 [64, 2048, 1024], P('owner', 'rows'), may hold values from -0.1875 to 0.1875
- avg_up: float32 [64, 2048, 1024], P('owner', 'rows'), may hold values from -0.125 to 0.125
- mix_share: float32 [64], P('owner'), may hold values from 0.2 to 0.8
- router_weight: float32 [2048, 64], P('rows', 'owner'), may hold values from -0.125 to 0.125
- router_gain: float32 [2048], P('rows'), may hold values from 0.25 to 1.75
Outputs:
- serve_gate: bfloat16 [64, 2048, 1024], P('owner')
- serve_up: bfloat16 [64, 2048, 1024], P('owner')
- scale_gate: float32 [64, 1024], P('owner')
- scale_up: float32 [64, 1024], P('owner')
- serve_router: bfloat16 [2048, 64], replicated
All inputs are finite; a program needn't handle non-finite values.
Results may differ from a plain program's by a relative error of at most 0.0015.
Values may be sent and summed in bfloat16 or wider, within the bound.
A program may use at most 64 MiB of HBM per device.

v0:
```python
import jax
import jax.numpy as jnp
from jax import lax
from jax.sharding import PartitionSpec as P


def copy_for_each(x, axis):
    length = lax.axis_size(axis)
    return lax.all_to_all(jnp.broadcast_to(x[None], (length, *x.shape)), axis, 0, 0, tiled=True)


def over_copies(x, axis):
    return copy_for_each(x, axis).sum(axis=0)


def packed_total(arrays, axis):
    vector, at, finished = (jnp.concatenate([a.reshape(-1) for a in arrays]), 0, [])
    so_far = over_copies(vector, axis)
    for a in arrays:
        finished.append(so_far[at : at + a.size].reshape(a.shape))
        at += a.size
    return tuple(finished)


def sent_together(arrays, axis, dim, along):
    ends, at = ([], 0)
    for a in arrays[:-1]:
        at += a.shape[along]
        ends.append(at)
    both = jnp.concatenate(arrays, axis=along)
    return tuple(jnp.split(lax.all_gather(both, axis, axis=dim, tiled=True), ends, axis=along))


def laid_out(tiles, dim):
    tiles = jnp.moveaxis(tiles, 0, dim)
    dims = tiles.shape
    return tiles.reshape(*dims[:dim], dims[dim] * dims[dim + 1], *dims[dim + 2 :])


def collect(x, axis, dim):
    tiles = copy_for_each(x, axis)
    return laid_out(tiles, dim)


def shards(w_gate, avg_gate, w_up, avg_up, mix_share, router_weight, router_gain):
    fresh_gate = mix_share[:, None, None] * w_gate + (1.0 - mix_share[:, None, None]) * avg_gate
    fresh_up = mix_share[:, None, None] * w_up + (1.0 - mix_share[:, None, None]) * avg_up
    total_gate, total_up = packed_total(
        (jnp.sum(fresh_gate * fresh_gate, axis=1), jnp.sum(fresh_up * fresh_up, axis=1)), "rows"
    )
    scale_gate = jnp.sqrt(total_gate)
    scale_up = jnp.sqrt(total_up)
    narrow_gate, narrow_up = (
        (fresh_gate / jnp.expand_dims(scale_gate, 1)).astype(jnp.bfloat16),
        (fresh_up / jnp.expand_dims(scale_up, 1)).astype(jnp.bfloat16),
    )
    serve_gate, serve_up = sent_together((narrow_gate, narrow_up), "rows", 1, 0)
    part_router = (router_weight * router_gain[:, None]).astype(jnp.bfloat16)
    row_router = collect(part_router, "rows", 0)
    serve_router = lax.all_gather(row_router, "owner", axis=1, tiled=True)
    return (serve_gate, serve_up, scale_gate, scale_up, serve_router)


def solution(mesh):
    placed = (
        P("owner", "rows", None),
        P("owner", "rows", None),
        P("owner", "rows", None),
        P("owner", "rows", None),
        P("owner"),
        P("rows", "owner"),
        P("rows"),
    )
    return jax.shard_map(
        shards,
        mesh=mesh,
        in_specs=placed,
        out_specs=(
            P("owner", None, None),
            P("owner", None, None),
            P("owner", None),
            P("owner", None),
            P(),
        ),
        check_vma=False,
    )
```

profile of v0, /device:TPU:1, one launch (start us, length us, event | category | flops | bytes accessed | tf_op | source)
XLA Modules:
  0.0 146.4 jit_solution(4776835904799485713)
XLA Ops:
  7.2 0.0 copy-start.2
  7.2 0.0 copy-start
  7.2 0.0 copy-start.1
  7.2 0.0 all-gather.3.cloned.1.call-start
  8.0 1.8 %multiply_reduce_fusion.1 = f32[1024]{0:T(1024)S(1)} fusion(f32[1,256,1024]{2,1,0:T(8,128)} %param.8, f32[]{:T(128)} %bitcast.1, f32[1,256,1024]{2,1,0:T(8,128)} %param.7, f32[]{:T(128)} %bitcast.14), kind=kLoop, calls=%fused_computation.5 | loop fusion | flops 1309696 | bytes 2101256 | tf_op jit(solution)/shard_map/reduce_sum | solution.py:49
  9.9 1.8 %multiply_reduce_fusion = f32[1024]{0:T(1024)S(1)} fusion(f32[1,256,1024]{2,1,0:T(8,128)} %param.10, f32[]{:T(128)} %bitcast.1, f32[1,256,1024]{2,1,0:T(8,128)} %param.9, f32[]{:T(128)} %bitcast.15), kind=kLoop, calls=%fused_computation.3 | loop fusion | flops 1309696 | bytes 2101256 | tf_op jit(solution)/shard_map/reduce_sum | solution.py:49
  11.7 11.2 %all_to_all.11 = f32[8,1,2048]{2,1,0:T(1,128)S(1)} all-to-all(f32[8,1,2048]{2,1,0:T(1,128)S(1)} %broadcast_in_dim.8), channel_id=1, replica_groups=mesh['owner'=64,'rows'=8] {'rows'}, dimensions={0} | all-to-all | bytes 131072 | tf_op jit(solution)/shard_map/all_to_all | solution.py:9
  22.9 0.1 reduce_sum.29
  22.9 0.0 copy-start.3
  23.0 0.0 copy-start.4
  23.0 0.0 copy-done.2
  23.0 0.0 copy-done
  23.0 0.0 copy-done.1
  23.0 0.0 copy-start.5
  23.0 0.0 copy-start.6
  23.0 1.7 %divide_convert_fusion = (bf16[1,256,1024]{2,1,0:T(8,128)(2,1)S(1)}, bf16[1,256,1024]{2,1,0:T(8,128)(2,1)S(1)}) fusion(f32[1024]{0:T(1024)S(1)} %get-tuple-element.8, f32[1,256,1024]{2,1,0:T(8,128)S(1)} %copy-done, f32[]{:T(128)} %bitcast.1, f32[1,256,1024]{2,1,0:T(8,128)S(1)} %copy-done.1, f32[]{:T(128)} %bitcast.16, f32[1024]{0:T(1024)S(1)} %get-tuple-element.7, ...), kind=kLoop, calls=%fused_computation.1 | loop fusion | flops 2621440 | bytes 5251080 | tf_op jit(solution)/shard_map/convert_element_type | solution.py:55
  24.8 1.1 pad_maximum_fusion
  25.8 0.0 all-gather.3.cloned.1.call-update
  25.9 0.0 copy-done.3
  25.9 0.0 copy-done.4
  25.9 0.0 copy-done.5
  25.9 0.0 copy-done.6
  25.9 0.5 broadcast.11
  26.4 0.7 reduce.5
  27.1 7.4 %all_to_all.12 = bf16[8,2,128]{2,1,0:T(2,128)(2,1)S(1)} all-to-all(bf16[8,2,128]{2,1,0:T(2,128)(2,1)S(1)} %reshape.55), channel_id=1, replica_groups=mesh['owner'=64,'rows'=8] {'rows'}, dimensions={0} | all-to-all | bytes 8192 | tf_op jit(solution)/shard_map/all_to_all | solution.py:9
  34.5 95.3 %all-gather = bf16[64,1,2048]{2,1,0:T(2,128)(2,1)S(1)} all-gather(bf16[1,1,2048]{2,1,0:T(2,128)(2,1)S(1)} %bitcast.18), channel_id=1, replica_groups=mesh['owner'=64,'rows'=8] {'owner'}, dimensions={0}, use_global_device_ids=true | all-gather | bytes 266240 | tf_op jit(solution)/shard_map/all_gather | solution.py:60
  129.8 0.9 copy.18
  130.7 2.8 %all-gather.3.cloned.1.call-done = bf16[2,2048,1024]{2,1,0:T(8,128)(2,1)} async-done(((bf16[2,256,1024]{2,1,0:T(8,128)(2,1)}), bf16[2,2048,1024]{2,1,0:T(8,128)(2,1)}) %all-gather.3.cloned.1.call-update) | async-done | bytes 8388624 | tf_op jit(solution)/shard_map/all_gather | solution.py:31
  133.5 6.0 %fusion = (bf16[1,2048,1024]{2,1,0:T(8,128)(2,1)}, bf16[1,2048,1024]{2,1,0:T(8,128)(2,1)}) fusion(bf16[2,2048,1024]{2,1,0:T(8,128)(2,1)} %all-gather.3.cloned.1.call-done), kind=kLoop, calls=%fused_computation.12 | loop fusion | bytes 16777216 | tf_op jit(solution)/shard_map/split | solution.py:31
  (7 shorter events, 0.1 us)
Async XLA Ops:
  7.2 15.8 %copy-start.2 = (f32[1,256,1024]{2,1,0:T(8,128)S(1)}, f32[1,256,1024]{2,1,0:T(8,128)}, u32[]{:S(2)}) copy-start(f32[1,256,1024]{2,1,0:T(8,128)} %param.8) | copy-start | bytes 3145732
  7.2 15.8 %copy-start = (f32[1,256,1024]{2,1,0:T(8,128)S(1)}, f32[1,256,1024]{2,1,0:T(8,128)}, u32[]{:S(2)}) copy-start(f32[1,256,1024]{2,1,0:T(8,128)} %param.10) | copy-start | bytes 3145732
  7.2 15.8 %copy-start.1 = (f32[1,256,1024]{2,1,0:T(8,128)S(1)}, f32[1,256,1024]{2,1,0:T(8,128)}, u32[]{:S(2)}) copy-start(f32[1,256,1024]{2,1,0:T(8,128)} %param.9) | copy-start | bytes 3145732
  7.2 126.3 %all-gather.3.cloned.1.call-start = ((), (), s32[]{:S(2)}) async-start(), calls=%async_computation.2 | async-start | bytes 9437184 | tf_op jit(solution)/shard_map/all_gather | solution.py:31
  22.9 2.9 %copy-start.3 = (f32[1024]{0:T(1024)}, f32[1024]{0:T(1024)S(1)}, u32[]{:S(2)}) copy-start(f32[1024]{0:T(1024)S(1)} %get-tuple-element.7) | copy-start | bytes 12292
  23.0 2.9 %copy-start.4 = (f32[1024]{0:T(1024)}, f32[1024]{0:T(1024)S(1)}, u32[]{:S(2)}) copy-start(f32[1024]{0:T(1024)S(1)} %get-tuple-element.8) | copy-start | bytes 12292
  23.0 2.9 %copy-start.5 = (f32[256,1]{0,1:T(1,128)S(1)}, f32[256,1]{0,1:T(1,128)}, u32[]{:S(2)}) copy-start(f32[256,1]{0,1:T(1,128)} %param.12) | copy-start | bytes 3076
  23.0 2.9 %copy-start.6 = (f32[256]{0:T(256)S(1)}, f32[256]{0:T(256)}, u32[]{:S(2)}) copy-start(f32[256]{0:T(256)} %param.13) | copy-start | bytes 3076
Sparse Core Ops, SparseCore 0:
  26.0 107.4 all-gather.2
where the time goes:
time: 147 us; the launch traced here: 146 us
  blocking collectives  114 us (78%)
  between operations  15 us (10%)
  local copies, waits for them, and re-layouts  7.51 us (5%)
  other arithmetic  7.14 us (5%)
  waiting for transfers between devices  2.84 us (2%)
    all_gather x1, blocking collectives, shards(): serve_router = lax.all_gather(row_router, 'owner', axis=1, tiled=True)  95.3 us
    all_to_all x2, blocking collectives, copy_for_each(): lax.all_to_all(jnp.broadcast_to(x[None], (length, *x.shape)), axis, 0, 0,...  18.6 us
    split x1, local copies, waits for them, and re-layouts, sent_together(): jnp.split(lax.all_gather(both, axis, axis=dim, tiled=True), ends, axis=al...  6.02 us
  transfers between devices with their start and end apart: 1, of which 1 were waited for; matrix products, arithmetic and copies ran while one was open for 1% of the time, Pallas kernels for 0%

commit v1 on v0

v1 whole, which is shorter than its diff:
```python
import functools

import jax
import jax.numpy as jnp
from jax import lax
from jax.experimental import pallas as pl
from jax.experimental.pallas import tpu as pltpu
from jax.sharding import PartitionSpec as P

SIDE = 4
STEP = 16
ACROSS = 9


def chunk_at(k, first):
    held = ACROSS if first else 16 - ACROSS
    return k // held, k % held + (0 if first else ACROSS)


def gather_kernel(mix, w_gate, avg_gate, w_up, avg_up, out, scale, fresh, other, stats, load, sent, stat_sent, stat_got, got):
    me = lax.axis_index("rows")
    x, z = me % SIDE, me // SIDE
    right, left = z * SIDE + (x + 1) % SIDE, z * SIDE + (x + SIDE - 1) % SIDE
    across = (1 - z) * SIDE + x
    far = z * SIDE + (x + 2) % SIDE
    share = fresh.shape[1]
    n_first, n_rest = 2 * ACROSS, 2 * (16 - ACROSS)

    loads = []
    for i, (source, target) in enumerate(
        ((w_gate, fresh.at[0]), (avg_gate, other.at[0]), (w_up, fresh.at[1]), (avg_up, other.at[1]))
    ):
        loads.append(pltpu.make_async_copy(source.at[0], target, load.at[i]))
        loads[-1].start()

    barrier = pltpu.get_barrier_semaphore()
    for hop in range(1, 2 * SIDE):
        pl.semaphore_signal(barrier, inc=1, device_id={"rows": (me + hop) % (2 * SIDE)}, device_id_type=pl.DeviceIdType.MESH)

    part = mix[0]
    for a in range(2):
        loads[2 * a].wait()
        loads[2 * a + 1].wait()

        def mixed(i, total):
            rows = pl.ds(pl.multiple_of(i * 8, 8), 8)
            value = part * fresh[a, rows, :] + (1.0 - part) * other[a, rows, :]
            fresh[a, rows, :] = value
            return total + value * value

        total = lax.fori_loop(0, share // 8, mixed, jnp.zeros((8, fresh.shape[2]), jnp.float32), unroll=4)
        stats[me, pl.ds(a, 1), :] = jnp.sum(total, axis=0, keepdims=True)

    pl.semaphore_wait(barrier, 2 * SIDE - 1)

    def stat_copy(hop):
        return pltpu.make_async_remote_copy(
            src_ref=stats.at[me],
            dst_ref=stats.at[me],
            send_sem=stat_sent.at[hop],
            recv_sem=stat_got.at[me],
            device_id={"rows": (me + hop) % (2 * SIDE)},
            device_id_type=pl.DeviceIdType.MESH,
        )

    for hop in range(1, 2 * SIDE):
        stat_copy(hop).start()
    for hop in range(1, 2 * SIDE):
        source = (me + hop) % (2 * SIDE)
        pltpu.make_async_copy(stats.at[source], stats.at[source], stat_got.at[source]).wait()
    total = stats[0]
    for source in range(1, 2 * SIDE):
        total = total + stats[source]
    scale[...] = jnp.sqrt(total)

    def place(source, a, i):
        return out.at[a, pl.ds(pl.multiple_of(source * share + i * STEP, STEP), STEP), :]

    def send(source, a, i, target, link):
        pltpu.make_async_remote_copy(
            src_ref=place(source, a, i),
            dst_ref=place(source, a, i),
            send_sem=sent.at[link],
            recv_sem=got.at[source, a * 16 + i],
            device_id={"rows": target},
            device_id_type=pl.DeviceIdType.MESH,
        ).start()

    def arrived(source, a, i):
        pltpu.make_async_copy(place(source, a, i), place(source, a, i), got.at[source, a * 16 + i]).wait()

    def settle(a, i):
        rows = pl.ds(pl.multiple_of(i * STEP, STEP), STEP)
        value = fresh[a, rows, :] / scale[pl.ds(a, 1), :]
        out[a, pl.ds(pl.multiple_of(me * share + i * STEP, STEP), STEP), :] = value.astype(jnp.bfloat16)

    def own_step(k, _):
        @pl.when(k < n_first)
        def _():
            settle(*chunk_at(k, True))

        @pl.when(k < n_rest)
        def _():
            settle(*chunk_at(k, False))

        @pl.when(k > 0)
        def _():
            a, i = chunk_at(k - 1, True)
            send(me, a, i, across, 2)

        @pl.when((k > 0) & (k <= n_rest))
        def _():
            a, i = chunk_at(k - 1, False)
            send(me, a, i, right, 0)
            send(me, a, i, left, 1)

        return 0

    lax.fori_loop(0, n_first + 1, own_step, 0)

    def own_next(k, _):
        a, i = chunk_at(k, True)
        send(me, a, i, right, 0)
        send(me, a, i, left, 1)

        @pl.when(k < n_rest)
        def _():
            a, i = chunk_at(k, False)
            send(me, a, i, across, 2)

        return 0

    lax.fori_loop(0, n_first, own_next, 0)

    def near(k, first, z_too, from_left, from_right):
        a, i = chunk_at(k, first)
        arrived(from_left, a, i)
        arrived(from_right, a, i)
        if z_too:
            send(from_left, a, i, across, 2)
            send(from_right, a, i, across, 2)

        @pl.when(k % 2 == 0)
        def _():
            send(from_left, a, i, right, 0)

        @pl.when(k % 2 == 1)
        def _():
            send(from_right, a, i, left, 1)

        return 0

    lax.fori_loop(0, n_rest, lambda k, _: near(k, False, True, left, right), 0)

    def from_across(k, _):
        a, i = chunk_at(k, True)
        arrived(across, a, i)
        send(across, a, i, right, 0)
        send(across, a, i, left, 1)
        return 0

    lax.fori_loop(0, n_first, from_across, 0)
    lax.fori_loop(0, n_first, lambda k, _: near(k, True, False, left, right), 0)

    def far_rest(k, _):
        a, i = chunk_at(k, False)
        arrived(far, a, i)
        send(far, a, i, across, 2)
        return 0

    lax.fori_loop(0, n_rest, far_rest, 0)

    def flip(r):
        return (r + SIDE) % (2 * SIDE)

    lax.fori_loop(0, n_first, lambda k, _: near(k, True, False, flip(left), flip(right)), 0)

    def last_first(k, _):
        a, i = chunk_at(k, True)
        arrived(far, a, i)
        arrived(flip(far), a, i)
        return 0

    lax.fori_loop(0, n_first, last_first, 0)

    def last_rest(k, _):
        a, i = chunk_at(k, False)
        for source in (across, flip(left), flip(right), flip(far)):
            arrived(source, a, i)
        return 0

    lax.fori_loop(0, n_rest, last_rest, 0)

    for hop in range(1, 2 * SIDE):
        stat_copy(hop).wait_send()
    on_x = (n_rest + n_first) + n_rest // 2 + n_first + n_first // 2 + n_first // 2
    on_z = n_first + n_rest + 3 * n_rest
    for link, count in ((0, on_x), (1, on_x), (2, on_z)):
        all_sent = out.at[0, pl.ds(0, count * STEP), :]
        pltpu.make_async_copy(all_sent, all_sent, sent.at[link]).wait()


def place_kernel(gathered, scale, serve_gate, serve_up, scale_gate, scale_up, done):
    copies = (
        pltpu.make_async_copy(gathered.at[pl.ds(0, 1)], serve_gate, done.at[0]),
        pltpu.make_async_copy(gathered.at[pl.ds(1, 1)], serve_up, done.at[1]),
        pltpu.make_async_copy(scale.at[pl.ds(0, 1)], scale_gate, done.at[2]),
        pltpu.make_async_copy(scale.at[pl.ds(1, 1)], scale_up, done.at[3]),
    )
    for copy in copies:
        copy.start()
    for copy in copies:
        copy.wait()


def shards(w_gate, avg_gate, w_up, avg_up, mix_share, router_weight, router_gain):
    _, share, width = w_gate.shape
    n = lax.axis_size("rows")
    in_hbm = pl.BlockSpec(memory_space=pltpu.HBM)
    in_vmem = pl.BlockSpec(memory_space=pltpu.VMEM)
    gathered, scale = pl.pallas_call(
        gather_kernel,
        out_shape=(
            jax.ShapeDtypeStruct((2, n * share, width), jnp.bfloat16),
            jax.ShapeDtypeStruct((2, width), jnp.float32),
        ),
        in_specs=[pl.BlockSpec(memory_space=pltpu.SMEM)] + [in_hbm] * 4,
        out_specs=(in_vmem, in_vmem),
        scratch_shapes=[
            pltpu.VMEM((2, share, width), jnp.float32),
            pltpu.VMEM((2, share, width), jnp.float32),
            pltpu.VMEM((n, 2, width), jnp.float32),
            pltpu.SemaphoreType.DMA((4,)),
            pltpu.SemaphoreType.DMA((3,)),
            pltpu.SemaphoreType.DMA((n,)),
            pltpu.SemaphoreType.DMA((n,)),
            pltpu.SemaphoreType.DMA((n, 32)),
        ],
        compiler_params=pltpu.CompilerParams(collective_id=0, has_side_effects=True, vmem_limit_bytes=32 * 2**20),
        name="gather",
    )(mix_share, *(pltpu.with_memory_space_constraint(w, pltpu.HBM) for w in (w_gate, avg_gate, w_up, avg_up)))
    serve_gate, serve_up, scale_gate, scale_up = pl.pallas_call(
        place_kernel,
        out_shape=(
            jax.ShapeDtypeStruct((1, n * share, width), jnp.bfloat16),
            jax.ShapeDtypeStruct((1, n * share, width), jnp.bfloat16),
            jax.ShapeDtypeStruct((1, width), jnp.float32),
            jax.ShapeDtypeStruct((1, width), jnp.float32),
        ),
        in_specs=[in_vmem, in_vmem],
        out_specs=(in_hbm,) * 4,
        scratch_shapes=[pltpu.SemaphoreType.DMA((4,))],
        compiler_params=pltpu.CompilerParams(vmem_limit_bytes=32 * 2**20),
        name="place",
    )(gathered, scale)
    part_router = (router_weight * router_gain[:, None]).astype(jnp.bfloat16)
    row_router = lax.all_gather(part_router, "rows", axis=0, tiled=True)
    serve_router = lax.all_gather(row_router, "owner", axis=1, tiled=True)
    return (serve_gate, serve_up, scale_gate, scale_up, serve_router)


def solution(mesh):
    placed = (
        P("owner", "rows", None),
        P("owner", "rows", None),
        P("owner", "rows", None),
        P("owner", "rows", None),
        P("owner"),
        P("rows", "owner"),
        P("rows"),
    )
    return jax.shard_map(
        shards,
        mesh=mesh,
        in_specs=placed,
        out_specs=(
            P("owner", None, None),
            P("owner", None, None),
            P("owner", None),
            P("owner", None),
            P(),
        ),
        check_vma=False,
    )
```

time: 147 us -> 179 us (1.22)
  Pallas kernels: 0 us -> 66.1 us
  between operations: 15 us -> 1.33 us
  other arithmetic: 7.14 us -> 0.01 us
  local copies, waits for them, and re-layouts: 7.51 us -> 0.87 us
  blocking collectives: 114 us -> 111 us
  waiting for transfers between devices: 2.84 us -> 0 us
    pallas_call x0 -> x2, Pallas kernels: none -> 66.1 us  [the longest x1 62.7 us: shards(): pl.pallas_call(gather_kernel, out_shape=(jax.ShapeDtypeStruct((2, n * sha...]
    all_to_all x2 -> x0, blocking collectives: 18.6 us -> none  [copy_for_each(): lax.all_to_all(jnp.broadcast_to(x[None], (length, *x.shape)), axis, 0, 0,...]
    all_gather x0 -> x1, blocking collectives: none -> 13.2 us  [shards(): row_router = lax.all_gather(part_router, 'rows', axis=0, tiled=True)]
    split x1 -> x0, local copies, waits for them, and re-layouts: 6.02 us -> none  [sent_together(): jnp.split(lax.all_gather(both, axis, axis=dim, tiled=True), ends, axis=al...]
    reduce_sum x3 -> x0, other arithmetic: 3.64 us -> none  [the longest x1 1.83 us: shards(): jnp.sum(fresh_gate * fresh_gate, axis=1)]
    all_gather x1 -> x0, waiting for transfers between devices: 2.83 us -> none  [sent_together(): lax.all_gather(both, axis, axis=dim, tiled=True)]
    all_gather x1, blocking collectives: 95.3 us -> 97.8 us  [shards(): serve_router = lax.all_gather(row_router, 'owner', axis=1, tiled=True)]
  transfers between devices with their start and end apart: 1 -> 0, of which waited for: 1 -> 0; matrix products, arithmetic and copies ran while one was open for 1% -> 0% of each run, Pallas kernels for 0% -> 0%
where the time goes in v1:
time: 179 us
  blocking collectives  111 us (62%)
  Pallas kernels  66.1 us (37%)
    all_gather x1, blocking collectives, shards(): serve_router = lax.all_gather(row_router, 'owner', axis=1, tiled=True)  97.8 us
    pallas_call x1, Pallas kernels, shards(): pl.pallas_call(gather_kernel, out_shape=(jax.ShapeDtypeStruct((2, n * sha...  62.7 us
    all_gather x1, blocking collectives, shards(): row_router = lax.all_gather(part_router, 'rows', axis=0, tiled=True)  13.2 us

profile of v1, /device:TPU:1, one launch (start us, length us, event | category | flops | bytes accessed | tf_op | source)
XLA Modules:
  0.0 179.3 jit_solution(20394208184501703)
XLA Ops:
  1.3 62.7 %gather.1 = (bf16[2,2048,1024]{2,1,0:T(8,128)(2,1)S(1)}, f32[2,1024]{1,0:T(2,128)S(1)}) custom-call(f32[1]{0:T(128)S(6)} %copy.15.mix, f32[1,256,1024]{2,1,0:T(8,128)} %w_gate.1, f32[1,256,1024]{2,1,0:T(8,128)} %avg_gate.1, f32[1,256,1024]{2,1,0:T(8,128)} %w_up.1, f32[1,256,1024]{2,1,0:T(8,128)} %avg_up.1), custom_call_target="tpu_custom_call" | custom-call | tf_op jit(solution)/shard_map/gather/pallas_call | solution.py:221
  64.0 0.0 copy-start
  64.0 0.0 copy-start.1
  64.0 3.4 %place.1 = (bf16[1,2048,1024]{2,1,0:T(8,128)(2,1)}, bf16[1,2048,1024]{2,1,0:T(8,128)(2,1)}, f32[1,1024]{1,0:T(1,128)}, f32[1,1024]{1,0:T(1,128)}) custom-call(bf16[2,2048,1024]{2,1,0:T(8,128)(2,1)S(1)} %get-tuple-element.11.gathered, f32[2,1024]{1,0:T(2,128)S(1)} %get-tuple-element.12.scale), custom_call_target="tpu_custom_call" | custom-call | tf_op jit(solution)/shard_map/place/pallas_call | solution.py:242
  67.5 0.0 copy-done
  67.5 0.0 copy-done.1
  67.5 13.2 %all_gather.6 = bf16[2048,1]{0,1:T(2,128)(2,1)S(1)} all-gather(bf16[256,1]{0,1:T(2,128)(2,1)S(1)} %multiply_convert_fusion), channel_id=1, replica_groups=mesh['owner'=64,'rows'=8] {'rows'}, dimensions={0}, use_global_device_ids=true | all-gather | bytes 4608 | tf_op jit(solution)/shard_map/all_gather | solution.py:257
  80.7 97.8 %all-gather = bf16[64,1,2048]{2,1,0:T(2,128)(2,1)S(1)} all-gather(bf16[1,1,2048]{2,1,0:T(2,128)(2,1)S(1)} %bitcast.8), channel_id=1, replica_groups=mesh['owner'=64,'rows'=8] {'owner'}, dimensions={0}, use_global_device_ids=true | all-gather | bytes 266240 | tf_op jit(solution)/shard_map/all_gather | solution.py:258
  178.5 0.9 copy.14
  (1 shorter events, 0.0 us)
Async XLA Ops:
  64.0 3.5 %copy-start = (f32[256,1]{0,1:T(1,128)S(1)}, f32[256,1]{0,1:T(1,128)}, u32[]{:S(2)}) copy-start(f32[256,1]{0,1:T(1,128)} %param.12) | copy-start | bytes 3076
  64.0 3.5 %copy-start.1 = (f32[256]{0:T(256)S(1)}, f32[256]{0:T(256)}, u32[]{:S(2)}) copy-start(f32[256]{0:T(256)} %param.13) | copy-start | bytes 3076

commit v2 on v1

--- a/solution.py
+++ b/solution.py
@@ -9,6 +9,7 @@
 
 SIDE = 4
 STEP = 16
+TALL, WIDE, CORES = 8, 4, 2
 ACROSS = 9
 
 
@@ -17,8 +18,16 @@
     return k // held, k % held + (0 if first else ACROSS)
 
 
-def gather_kernel(mix, w_gate, avg_gate, w_up, avg_up, out, scale, fresh, other, stats, load, sent, stat_sent, stat_got, got):
+def gather_kernel(
+    mix, w_gate, avg_gate, w_up, avg_up, weight, gain,
+    out, scale, router,
+    fresh, other, stats, line, land, block,
+    load, sent, stat_sent, stat_got, got,
+    line_sent, line_got, ring_sent, ring_got, wide_sent, wide_got, core_sent, core_got,
+):
     me = lax.axis_index("rows")
+    owner = lax.axis_index("owner")
+    high, y, core = owner // (WIDE * CORES), owner // CORES % WIDE, owner % CORES
     x, z = me % SIDE, me // SIDE
     right, left = z * SIDE + (x + 1) % SIDE, z * SIDE + (x + SIDE - 1) % SIDE
     across = (1 - z) * SIDE + x
@@ -26,16 +35,32 @@
     share = fresh.shape[1]
     n_first, n_rest = 2 * ACROSS, 2 * (16 - ACROSS)
 
+    def at_owner(h, j, c):
+        return {"owner": (h * WIDE + j) * CORES + c}
+
     loads = []
     for i, (source, target) in enumerate(
-        ((w_gate, fresh.at[0]), (avg_gate, other.at[0]), (w_up, fresh.at[1]), (avg_up, other.at[1]))
+        (
+            (w_gate.at[0], fresh.at[0]),
+            (avg_gate.at[0], other.at[0]),
+            (w_up.at[0], fresh.at[1]),
+            (avg_up.at[0], other.at[1]),
+            (weight, line.at[0]),
+            (gain, line.at[1]),
+        )
     ):
-        loads.append(pltpu.make_async_copy(source.at[0], target, load.at[i]))
+        loads.append(pltpu.make_async_copy(source, target, load.at[i]))
         loads[-1].start()
 
     barrier = pltpu.get_barrier_semaphore()
     for hop in range(1, 2 * SIDE):
         pl.semaphore_signal(barrier, inc=1, device_id={"rows": (me + hop) % (2 * SIDE)}, device_id_type=pl.DeviceIdType.MESH)
+
+    others = [at_owner((high + hop) % TALL, y, core) for hop in (1, TALL - 1)]
+    others += [at_owner(high, (y + hop) % WIDE, core) for hop in range(1, WIDE)]
+    others.append(at_owner(high, y, 1 - core))
+    for target in others:
+        pl.semaphore_signal(barrier, inc=1, device_id=target, device_id_type=pl.DeviceIdType.MESH)
 
     part = mix[0]
     for a in range(2):
@@ -51,7 +76,12 @@
         total = lax.fori_loop(0, share // 8, mixed, jnp.zeros((8, fresh.shape[2]), jnp.float32), unroll=4)
         stats[me, pl.ds(a, 1), :] = jnp.sum(total, axis=0, keepdims=True)
 
-    pl.semaphore_wait(barrier, 2 * SIDE - 1)
+    loads[4].wait()
+    loads[5].wait()
+    lanes = pl.ds(pl.multiple_of(me * share, share), share)
+    land[high, y, core, :, lanes] = (line[0] * line[1]).astype(jnp.bfloat16).astype(jnp.float32)
+
+    pl.semaphore_wait(barrier, 2 * SIDE - 1 + len(others))
 
     def stat_copy(hop):
         return pltpu.make_async_remote_copy(
@@ -63,8 +93,53 @@
             device_id_type=pl.DeviceIdType.MESH,
         )
 
+    def remote(place, send_sem, recv_sem, target):
+        return pltpu.make_async_remote_copy(
+            src_ref=place,
+            dst_ref=place,
+            send_sem=send_sem,
+            recv_sem=recv_sem,
+            device_id=target,
+            device_id_type=pl.DeviceIdType.MESH,
+        )
+
+    def line_place(source):
+        return land.at[high, y, core, :, pl.ds(pl.multiple_of(source * share, share), share)]
+
+    def line_copy(hop):
+        return remote(line_place(me), line_sent.at[hop], line_got.at[me], {"rows": (me + hop) % (2 * SIDE)})
+
+    def ring_copy(way, step):
+        towards = 1 if way == 0 else TALL - 1
+        tile = (high + (TALL - towards) * step) % TALL
+        target = at_owner((high + towards) % TALL, y, core)
+        return remote(land.at[tile, y, core], ring_sent.at[way, step], ring_got.at[way, step], target)
+
+    def ring_wait(way, step):
+        towards = 1 if way == 0 else TALL - 1
+        tile = land.at[(high + (TALL - towards) * (step + 1)) % TALL, y, core]
+        pltpu.make_async_copy(tile, tile, ring_got.at[way, step]).wait()
+
+    steps = (TALL // 2, (TALL - 1) // 2)
+
+    def ring_step(step):
+        for way in range(2):
+            if 0 < step <= steps[way]:
+                ring_wait(way, step - 1)
+            if step < steps[way]:
+                ring_copy(way, step).start()
+
+    def wide_copy(hop):
+        target = at_owner(high, (y + hop) % WIDE, core)
+        return remote(land.at[:, y, core], wide_sent.at[hop], wide_got.at[y], target)
+
+    def core_copy():
+        return remote(land.at[:, :, core], core_sent.at[0], core_got.at[0], at_owner(high, y, 1 - core))
+
     for hop in range(1, 2 * SIDE):
         stat_copy(hop).start()
+    for hop in range(1, 2 * SIDE):
+        line_copy(hop).start()
     for hop in range(1, 2 * SIDE):
         source = (me + hop) % (2 * SIDE)
         pltpu.make_async_copy(stats.at[source], stats.at[source], stat_got.at[source]).wait()
@@ -94,43 +169,30 @@
         value = fresh[a, rows, :] / scale[pl.ds(a, 1), :]
         out[a, pl.ds(pl.multiple_of(me * share + i * STEP, STEP), STEP), :] = value.astype(jnp.bfloat16)
 
-    def own_step(k, _):
-        @pl.when(k < n_first)
-        def _():
-            settle(*chunk_at(k, True))
-
-        @pl.when(k < n_rest)
-        def _():
-            settle(*chunk_at(k, False))
-
-        @pl.when(k > 0)
-        def _():
-            a, i = chunk_at(k - 1, True)
-            send(me, a, i, across, 2)
-
-        @pl.when((k > 0) & (k <= n_rest))
-        def _():
-            a, i = chunk_at(k - 1, False)
-            send(me, a, i, right, 0)
-            send(me, a, i, left, 1)
-
-        return 0
-
-    lax.fori_loop(0, n_first + 1, own_step, 0)
-
-    def own_next(k, _):
-        a, i = chunk_at(k, True)
+    paced = (6, 12, 18, 25, 32)
+
+    def own_send(k):
+        a, i = chunk_at(k, False) if k < n_rest else chunk_at(k - n_rest, True)
         send(me, a, i, right, 0)
         send(me, a, i, left, 1)
-
-        @pl.when(k < n_rest)
-        def _():
-            a, i = chunk_at(k, False)
-            send(me, a, i, across, 2)
-
-        return 0
-
-    lax.fori_loop(0, n_first, own_next, 0)
+        a, i = chunk_at(k, True) if k < n_first else chunk_at(k - n_first, False)
+        send(me, a, i, across, 2)
+
+    for k in range(n_first + 1):
+        if k < n_first:
+            settle(*chunk_at(k, True))
+        if k < n_rest:
+            settle(*chunk_at(k, False))
+        if 0 < k <= paced[0]:
+            own_send(k - 1)
+
+    for hop in range(1, 2 * SIDE):
+        source = (me + hop) % (2 * SIDE)
+        pltpu.make_async_copy(line_place(source), line_place(source), line_got.at[source]).wait()
+    for step in range(len(paced) - 1):
+        ring_step(step)
+        for k in range(paced[step], paced[step + 1]):
+            own_send(k)
 
     def near(k, first, z_too, from_left, from_right):
         a, i = chunk_at(k, first)
@@ -152,6 +214,11 @@
 
     lax.fori_loop(0, n_rest, lambda k, _: near(k, False, True, left, right), 0)
 
+    for step in range(len(paced) - 1, steps[0] + 1):
+        ring_step(step)
+    for hop in range(1, WIDE):
+        wide_copy(hop).start()
+
     def from_across(k, _):
         a, i = chunk_at(k, True)
         arrived(across, a, i)
@@ -162,6 +229,11 @@
     lax.fori_loop(0, n_first, from_across, 0)
     lax.fori_loop(0, n_first, lambda k, _: near(k, True, False, left, right), 0)
 
+    for hop in range(1, WIDE):
+        source = land.at[:, (y + hop) % WIDE, core]
+        pltpu.make_async_copy(source, source, wide_got.at[(y + hop) % WIDE]).wait()
+    core_copy().start()
+
     def far_rest(k, _):
         a, i = chunk_at(k, False)
         arrived(far, a, i)
@@ -175,6 +247,18 @@
 
     lax.fori_loop(0, n_first, lambda k, _: near(k, True, False, flip(left), flip(right)), 0)
 
+    theirs = land.at[:, :, 1 - core]
+    pltpu.make_async_copy(theirs, theirs, core_got.at[0]).wait()
+    for first in range(0, TALL * WIDE * CORES, 16):
+
+        def line_in(k, _):
+            o = first + k
+            block[pl.ds(k, 1), :] = land[o // (WIDE * CORES), o // CORES % WIDE, o % CORES]
+            return 0
+
+        lax.fori_loop(0, 16, line_in, 0)
+        router[pl.ds(first, 16), :] = block[...].astype(jnp.bfloat16)
+
     def last_first(k, _):
         a, i = chunk_at(k, True)
         arrived(far, a, i)
@@ -193,6 +277,13 @@
 
     for hop in range(1, 2 * SIDE):
         stat_copy(hop).wait_send()
+        line_copy(hop).wait_send()
+    for way in range(2):
+        for step in range(steps[way]):
+            ring_copy(way, step).wait_send()
+    for hop in range(1, WIDE):
+        wide_copy(hop).wait_send()
+    core_copy().wait_send()
     on_x = (n_rest + n_first) + n_rest // 2 + n_first + n_first // 2 + n_first // 2
     on_z = n_first + n_rest + 3 * n_rest
     for link, count in ((0, on_x), (1, on_x), (2, on_z)):
@@ -200,12 +291,13 @@
         pltpu.make_async_copy(all_sent, all_sent, sent.at[link]).wait()
 
 
-def place_kernel(gathered, scale, serve_gate, serve_up, scale_gate, scale_up, done):
+def place_kernel(gathered, scale, router, serve_gate, serve_up, scale_gate, scale_up, serve_router, done):
     copies = (
         pltpu.make_async_copy(gathered.at[pl.ds(0, 1)], serve_gate, done.at[0]),
         pltpu.make_async_copy(gathered.at[pl.ds(1, 1)], serve_up, done.at[1]),
         pltpu.make_async_copy(scale.at[pl.ds(0, 1)], scale_gate, done.at[2]),
         pltpu.make_async_copy(scale.at[pl.ds(1, 1)], scale_up, done.at[3]),
+        pltpu.make_async_copy(router, serve_router, done.at[4]),
     )
     for copy in copies:
         copy.start()
@@ -218,45 +310,57 @@
     n = lax.axis_size("rows")
     in_hbm = pl.BlockSpec(memory_space=pltpu.HBM)
     in_vmem = pl.BlockSpec(memory_space=pltpu.VMEM)
-    gathered, scale = pl.pallas_call(
+    held = (w_gate, avg_gate, w_up, avg_up, router_weight.T, router_gain[None])
+    owners = TALL * WIDE * CORES
+    gathered, scale, router = pl.pallas_call(
         gather_kernel,
         out_shape=(
             jax.ShapeDtypeStruct((2, n * share, width), jnp.bfloat16),
             jax.ShapeDtypeStruct((2, width), jnp.float32),
+            jax.ShapeDtypeStruct((owners, n * share), jnp.bfloat16),
         ),
-        in_specs=[pl.BlockSpec(memory_space=pltpu.SMEM)] + [in_hbm] * 4,
-        out_specs=(in_vmem, in_vmem),
+        in_specs=[pl.BlockSpec(memory_space=pltpu.SMEM)] + [in_hbm] * 6,
+        out_specs=(in_vmem,) * 3,
         scratch_shapes=[
             pltpu.VMEM((2, share, width), jnp.float32),
             pltpu.VMEM((2, share, width), jnp.float32),
             pltpu.VMEM((n, 2, width), jnp.float32),
-            pltpu.SemaphoreType.DMA((4,)),
+            pltpu.VMEM((2, 1, share), jnp.float32),
+            pltpu.VMEM((TALL, WIDE, CORES, 1, n * share), jnp.float32),
+            pltpu.VMEM((16, n * share), jnp.float32),
+            pltpu.SemaphoreType.DMA((6,)),
             pltpu.SemaphoreType.DMA((3,)),
             pltpu.SemaphoreType.DMA((n,)),
             pltpu.SemaphoreType.DMA((n,)),
             pltpu.SemaphoreType.DMA((n, 32)),
+            pltpu.SemaphoreType.DMA((n,)),
+            pltpu.SemaphoreType.DMA((n,)),
+            pltpu.SemaphoreType.DMA((2, TALL // 2)),
+            pltpu.SemaphoreType.DMA((2, TALL // 2)),
+            pltpu.SemaphoreType.DMA((WIDE,)),
+            pltpu.SemaphoreType.DMA((WIDE,)),
+            pltpu.SemaphoreType.DMA((1,)),
+            pltpu.SemaphoreType.DMA((1,)),
         ],
         compiler_params=pltpu.CompilerParams(collective_id=0, has_side_effects=True, vmem_limit_bytes=32 * 2**20),
         name="gather",
-    )(mix_share, *(pltpu.with_memory_space_constraint(w, pltpu.HBM) for w in (w_gate, avg_gate, w_up, avg_up)))
-    serve_gate, serve_up, scale_gate, scale_up = pl.pallas_call(
+    )(mix_share, *(pltpu.with_memory_space_constraint(w, pltpu.HBM) for w in held))
+    serve_gate, serve_up, scale_gate, scale_up, serve_router = pl.pallas_call(
         place_kernel,
         out_shape=(
             jax.ShapeDtypeStruct((1, n * share, width), jnp.bfloat16),
             jax.ShapeDtypeStruct((1, n * share, width), jnp.bfloat16),
             jax.ShapeDtypeStruct((1, width), jnp.float32),
             jax.ShapeDtypeStruct((1, width), jnp.float32),
+            jax.ShapeDtypeStruct((owners, n * share), jnp.bfloat16),
         ),
-        in_specs=[in_vmem, in_vmem],
-        out_specs=(in_hbm,) * 4,
-        scratch_shapes=[pltpu.SemaphoreType.DMA((4,))],
+        in_specs=[in_vmem] * 3,
+        out_specs=(in_hbm,) * 5,
+        scratch_shapes=[pltpu.SemaphoreType.DMA((5,))],
         compiler_params=pltpu.CompilerParams(vmem_limit_bytes=32 * 2**20),
         name="place",
-    )(gathered, scale)
-    part_router = (router_weight * router_gain[:, None]).astype(jnp.bfloat16)
-    row_router = lax.all_gather(part_router, "rows", axis=0, tiled=True)
-    serve_router = lax.all_gather(row_router, "owner", axis=1, tiled=True)
-    return (serve_gate, serve_up, scale_gate, scale_up, serve_router)
+    )(gathered, scale, router)
+    return (serve_gate, serve_up, scale_gate, scale_up, serve_router.T)
 
 
 def solution(mesh):

time: 179 us -> 77.8 us (0.43)
  blocking collectives: 111 us -> 0 us
  Pallas kernels: 66.1 us -> 75.2 us
    all_gather x2 -> x0, blocking collectives: 111 us -> none  [the longest x1 97.8 us: shards(): serve_router = lax.all_gather(row_router, 'owner', axis=1, tiled=True)]
    pallas_call x1, Pallas kernels: 62.7 us -> 71.8 us  [shards(): pl.pallas_call(gather_kernel, out_shape=(jax.ShapeDtypeStruct((2, n * sha...]
where the time goes in v2:
time: 77.8 us; the launch traced here: 76.5 us
  Pallas kernels  75.2 us (97%)
  between operations  1.29 us (2%)
    pallas_call x1, Pallas kernels, shards(): pl.pallas_call(gather_kernel, out_shape=(jax.ShapeDtypeStruct((2, n * sha...  71.8 us
    pallas_call x1, Pallas kernels, shards(): pl.pallas_call(place_kernel, out_shape=(jax.ShapeDtypeStruct((1, n * shar...  3.45 us

profile of v2, /device:TPU:1, one launch (start us, length us, event | category | flops | bytes accessed | tf_op | source)
XLA Modules:
  0.0 76.5 jit_solution(17709653074722259987)
XLA Ops:
  1.3 71.8 %gather.1 = (bf16[2,2048,1024]{2,1,0:T(8,128)(2,1)S(1)}, f32[2,1024]{1,0:T(2,128)S(1)}, bf16[64,2048]{1,0:T(8,128)(2,1)S(1)}) custom-call(f32[1]{0:T(128)S(6)} %copy.12.mix, f32[1,256,1024]{2,1,0:T(8,128)} %w_gate.1, f32[1,256,1024]{2,1,0:T(8,128)} %avg_gate.1, f32[1,256,1024]{2,1,0:T(8,128)} %w_up.1, f32[1,256,1024]{2,1,0:T(8,128)} %avg_up.1, ...), custom_call_target="tpu_custom_call" | custom-call | tf_op jit(solution)/shard_map/gather/pallas_call | solution.py:315
  73.1 3.4 %place.1 = (bf16[1,2048,1024]{2,1,0:T(8,128)(2,1)}, bf16[1,2048,1024]{2,1,0:T(8,128)(2,1)}, f32[1,1024]{1,0:T(1,128)}, f32[1,1024]{1,0:T(1,128)}, bf16[64,2048]{1,0:T(8,128)(2,1)}) custom-call(bf16[2,2048,1024]{2,1,0:T(8,128)(2,1)S(1)} %get-tuple-element.13.gathered, f32[2,1024]{1,0:T(2,128)S(1)} %get-tuple-element.14.scale, ...), custom_call_target="tpu_custom_call" | custom-call | tf_op jit(solution)/shard_map/place/pallas_call | solution.py:348

commit v3 on v2

--- a/solution.py
+++ b/solution.py
@@ -10,6 +10,8 @@
 SIDE = 4
 STEP = 16
 TALL, WIDE, CORES = 8, 4, 2
+BEHIND = 8
+APART = 11
 ACROSS = 9
 
 
@@ -169,111 +171,93 @@
         value = fresh[a, rows, :] / scale[pl.ds(a, 1), :]
         out[a, pl.ds(pl.multiple_of(me * share + i * STEP, STEP), STEP), :] = value.astype(jnp.bfloat16)
 
-    paced = (6, 12, 18, 25, 32)
-
-    def own_send(k):
-        a, i = chunk_at(k, False) if k < n_rest else chunk_at(k - n_rest, True)
-        send(me, a, i, right, 0)
-        send(me, a, i, left, 1)
-        a, i = chunk_at(k, True) if k < n_first else chunk_at(k - n_first, False)
-        send(me, a, i, across, 2)
-
-    for k in range(n_first + 1):
-        if k < n_first:
-            settle(*chunk_at(k, True))
-        if k < n_rest:
-            settle(*chunk_at(k, False))
-        if 0 < k <= paced[0]:
-            own_send(k - 1)
-
-    for hop in range(1, 2 * SIDE):
-        source = (me + hop) % (2 * SIDE)
-        pltpu.make_async_copy(line_place(source), line_place(source), line_got.at[source]).wait()
-    for step in range(len(paced) - 1):
-        ring_step(step)
-        for k in range(paced[step], paced[step + 1]):
-            own_send(k)
-
-    def near(k, first, z_too, from_left, from_right):
-        a, i = chunk_at(k, first)
-        arrived(from_left, a, i)
-        arrived(from_right, a, i)
-        if z_too:
-            send(from_left, a, i, across, 2)
-            send(from_right, a, i, across, 2)
-
-        @pl.when(k % 2 == 0)
-        def _():
-            send(from_left, a, i, right, 0)
-
-        @pl.when(k % 2 == 1)
-        def _():
-            send(from_right, a, i, left, 1)
-
-        return 0
-
-    lax.fori_loop(0, n_rest, lambda k, _: near(k, False, True, left, right), 0)
-
-    for step in range(len(paced) - 1, steps[0] + 1):
-        ring_step(step)
-    for hop in range(1, WIDE):
-        wide_copy(hop).start()
-
-    def from_across(k, _):
-        a, i = chunk_at(k, True)
-        arrived(across, a, i)
-        send(across, a, i, right, 0)
-        send(across, a, i, left, 1)
-        return 0
-
-    lax.fori_loop(0, n_first, from_across, 0)
-    lax.fori_loop(0, n_first, lambda k, _: near(k, True, False, left, right), 0)
-
-    for hop in range(1, WIDE):
-        source = land.at[:, (y + hop) % WIDE, core]
-        pltpu.make_async_copy(source, source, wide_got.at[(y + hop) % WIDE]).wait()
-    core_copy().start()
-
-    def far_rest(k, _):
-        a, i = chunk_at(k, False)
-        arrived(far, a, i)
-        send(far, a, i, across, 2)
-        return 0
-
-    lax.fori_loop(0, n_rest, far_rest, 0)
-
     def flip(r):
         return (r + SIDE) % (2 * SIDE)
 
-    lax.fori_loop(0, n_first, lambda k, _: near(k, True, False, flip(left), flip(right)), 0)
-
-    theirs = land.at[:, :, 1 - core]
-    pltpu.make_async_copy(theirs, theirs, core_got.at[0]).wait()
-    for first in range(0, TALL * WIDE * CORES, 16):
-
-        def line_in(k, _):
-            o = first + k
-            block[pl.ds(k, 1), :] = land[o // (WIDE * CORES), o // CORES % WIDE, o % CORES]
-            return 0
-
-        lax.fori_loop(0, 16, line_in, 0)
-        router[pl.ds(first, 16), :] = block[...].astype(jnp.bfloat16)
-
-    def last_first(k, _):
-        a, i = chunk_at(k, True)
-        arrived(far, a, i)
-        arrived(flip(far), a, i)
-        return 0
-
-    lax.fori_loop(0, n_first, last_first, 0)
-
-    def last_rest(k, _):
-        a, i = chunk_at(k, False)
-        for source in (across, flip(left), flip(right), flip(far)):
-            arrived(source, a, i)
-        return 0
-
-    lax.fori_loop(0, n_rest, last_rest, 0)
+    firsts = [chunk_at(k, True) for k in range(n_first)]
+    rests = [chunk_at(k, False) for k in range(n_rest)]
+
+    def round_x(near, way):
+        return (
+            [(me, c) for c in rests]
+            + [(me, c) for c in firsts]
+            + [(near, c) for c in rests[way::2]]
+            + [(across, c) for c in firsts]
+            + [(near, c) for c in firsts[way::2]]
+            + [(flip(near), c) for c in firsts[way::2]]
+        )
+
+    def from_x(near, way):
+        return (
+            [(near, c) for c in rests]
+            + [(near, c) for c in firsts]
+            + [(far, c) for c in rests[way::2]]
+            + [(flip(near), c) for c in firsts]
+            + [(far, c) for c in firsts[way::2]]
+            + [(flip(far), c) for c in firsts[way::2]]
+        )
+
+    def over_z(own, one, two, three):
+        return [(own, c) for c in firsts] + [(own, c) for c in rests] + [(r, c) for r in (one, two, three) for c in rests]
+
+    goes = (round_x(left, 0), round_x(right, 1), over_z(me, left, right, far))
+    comes = (from_x(left, 0), from_x(right, 1), over_z(across, flip(left), flip(right), flip(far)))
+    targets = (right, left, across)
+    slots = max(len(g) for g in goes)
+
+    def line_wait():
+        for hop in range(1, 2 * SIDE):
+            source = (me + hop) % (2 * SIDE)
+            pltpu.make_async_copy(line_place(source), line_place(source), line_got.at[source]).wait()
+
+    def wide_wait():
+        for hop in range(1, WIDE):
+            source = land.at[:, (y + hop) % WIDE, core]
+            pltpu.make_async_copy(source, source, wide_got.at[(y + hop) % WIDE]).wait()
+
+    def router_step(step):
+        if step == 0:
+            line_wait()
+        if step <= steps[0]:
+            ring_step(step)
+        if step == steps[0]:
+            for hop in range(1, WIDE):
+                wide_copy(hop).start()
+        if step == steps[0] + 1:
+            wide_wait()
+            core_copy().start()
+        if step == steps[0] + 2:
+            theirs = land.at[:, :, 1 - core]
+            pltpu.make_async_copy(theirs, theirs, core_got.at[0]).wait()
+            for first in range(0, TALL * WIDE * CORES, 16):
+
+                def line_in(k, _):
+                    o = first + k
+                    block[pl.ds(k, 1), :] = land[o // (WIDE * CORES), o // CORES % WIDE, o % CORES]
+                    return 0
+
+                lax.fori_loop(0, 16, line_in, 0)
+                router[pl.ds(first, 16), :] = block[...].astype(jnp.bfloat16)
+
+    def settle_pair(k):
+        for chunks in (firsts, rests):
+            if k < len(chunks):
+                settle(*chunks[k])
+
+    settle_pair(0)
+    for slot in range(slots + BEHIND):
+        settle_pair(slot + 1)
+        if slot >= BEHIND:
+            for came in comes:
+                if slot - BEHIND < len(came):
+                    source, (a, i) = came[slot - BEHIND]
+                    arrived(source, a, i)
+        for link in range(3):
+            if slot < len(goes[link]):
+                source, (a, i) = goes[link][slot]
+                send(source, a, i, targets[link], link)
+        if slot % APART == APART // 2 and slot // APART <= steps[0] + 2:
+            router_step(slot // APART)
 
     for hop in range(1, 2 * SIDE):
         stat_copy(hop).wait_send()
@@ -284,9 +268,8 @@
     for hop in range(1, WIDE):
         wide_copy(hop).wait_send()
     core_copy().wait_send()
-    on_x = (n_rest + n_first) + n_rest // 2 + n_first + n_first // 2 + n_first // 2
-    on_z = n_first + n_rest + 3 * n_rest
-    for link, count in ((0, on_x), (1, on_x), (2, on_z)):
+    for link in range(3):
+        count = len(goes[link])
         all_sent = out.at[0, pl.ds(0, count * STEP), :]
         pltpu.make_async_copy(all_sent, all_sent, sent.at[link]).wait()
 

time: 77.8 us -> 77.5 us (level)
  no operation moved by 1% of the time
where the time goes in v3:
time: 77.5 us; the launch traced here: 76.2 us
  Pallas kernels  74.9 us (97%)
  between operations  1.29 us (2%)
    pallas_call x1, Pallas kernels, shards(): pl.pallas_call(gather_kernel, out_shape=(jax.ShapeDtypeStruct((2, n * sha...  71.5 us
    pallas_call x1, Pallas kernels, shards(): pl.pallas_call(place_kernel, out_shape=(jax.ShapeDtypeStruct((1, n * shar...  3.45 us

profile of v3, /device:TPU:1, one launch (start us, length us, event | category | flops | bytes accessed | tf_op | source)
XLA Modules:
  0.0 76.2 jit_solution(3172580679262108726)
XLA Ops:
  1.3 71.5 %gather.1 = (bf16[2,2048,1024]{2,1,0:T(8,128)(2,1)S(1)}, f32[2,1024]{1,0:T(2,128)S(1)}, bf16[64,2048]{1,0:T(8,128)(2,1)S(1)}) custom-call(f32[1]{0:T(128)S(6)} %copy.12.mix, f32[1,256,1024]{2,1,0:T(8,128)} %w_gate.1, f32[1,256,1024]{2,1,0:T(8,128)} %avg_gate.1, f32[1,256,1024]{2,1,0:T(8,128)} %w_up.1, f32[1,256,1024]{2,1,0:T(8,128)} %avg_up.1, ...), custom_call_target="tpu_custom_call" | custom-call | tf_op jit(solution)/shard_map/gather/pallas_call | solution.py:298
  72.8 3.4 %place.1 = (bf16[1,2048,1024]{2,1,0:T(8,128)(2,1)}, bf16[1,2048,1024]{2,1,0:T(8,128)(2,1)}, f32[1,1024]{1,0:T(1,128)}, f32[1,1024]{1,0:T(1,128)}, bf16[64,2048]{1,0:T(8,128)(2,1)}) custom-call(bf16[2,2048,1024]{2,1,0:T(8,128)(2,1)S(1)} %get-tuple-element.13.gathered, f32[2,1024]{1,0:T(2,128)S(1)} %get-tuple-element.14.scale, ...), custom_call_target="tpu_custom_call" | custom-call | tf_op jit(solution)/shard_map/place/pallas_call | solution.py:331

commit v4 on v3

--- a/solution.py
+++ b/solution.py
@@ -10,8 +10,8 @@
 SIDE = 4
 STEP = 16
 TALL, WIDE, CORES = 8, 4, 2
-BEHIND = 8
-APART = 11
+BEHIND = 6
+APART = 7
 ACROSS = 9
 
 
@@ -25,7 +25,7 @@
     out, scale, router,
     fresh, other, stats, line, land, block,
     load, sent, stat_sent, stat_got, got,
-    line_sent, line_got, ring_sent, ring_got, wide_sent, wide_got, core_sent, core_got,
+    line_sent, line_got, z_sent, z_got, wide_sent, wide_got, core_sent, core_got,
 ):
     me = lax.axis_index("rows")
     owner = lax.axis_index("owner")
@@ -58,8 +58,15 @@
     for hop in range(1, 2 * SIDE):
         pl.semaphore_signal(barrier, inc=1, device_id={"rows": (me + hop) % (2 * SIDE)}, device_id_type=pl.DeviceIdType.MESH)
 
-    others = [at_owner((high + hop) % TALL, y, core) for hop in (1, TALL - 1)]
-    others += [at_owner(high, (y + hop) % WIDE, core) for hop in range(1, WIDE)]
+    above, below = high < TALL - 1, high > 0
+    for there, step in ((above, 1), (below, -1)):
+
+        @pl.when(there)
+        def _():
+            target = at_owner(high + step, y, core)
+            pl.semaphore_signal(barrier, inc=1, device_id=target, device_id_type=pl.DeviceIdType.MESH)
+
+    others = [at_owner(high, (y + hop) % WIDE, core) for hop in range(1, WIDE)]
     others.append(at_owner(high, y, 1 - core))
     for target in others:
         pl.semaphore_signal(barrier, inc=1, device_id=target, device_id_type=pl.DeviceIdType.MESH)
@@ -83,7 +90,8 @@
     lanes = pl.ds(pl.multiple_of(me * share, share), share)
     land[high, y, core, :, lanes] = (line[0] * line[1]).astype(jnp.bfloat16).astype(jnp.float32)
 
-    pl.semaphore_wait(barrier, 2 * SIDE - 1 + len(others))
+    greeted = 2 * SIDE - 1 + len(others) + above.astype(jnp.int32) + below.astype(jnp.int32)
+    pl.semaphore_wait(barrier, greeted)
 
     def stat_copy(hop):
         return pltpu.make_async_remote_copy(
@@ -111,25 +119,31 @@
     def line_copy(hop):
         return remote(line_place(me), line_sent.at[hop], line_got.at[me], {"rows": (me + hop) % (2 * SIDE)})
 
-    def ring_copy(way, step):
-        towards = 1 if way == 0 else TALL - 1
-        tile = (high + (TALL - towards) * step) % TALL
-        target = at_owner((high + towards) % TALL, y, core)
-        return remote(land.at[tile, y, core], ring_sent.at[way, step], ring_got.at[way, step], target)
-
-    def ring_wait(way, step):
-        towards = 1 if way == 0 else TALL - 1
-        tile = land.at[(high + (TALL - towards) * (step + 1)) % TALL, y, core]
-        pltpu.make_async_copy(tile, tile, ring_got.at[way, step]).wait()
-
-    steps = (TALL // 2, (TALL - 1) // 2)
-
-    def ring_step(step):
+    def z_copy(way, step):
+        towards = 1 - 2 * way
+        target = at_owner(high + towards, y, core)
+        return remote(land.at[high - towards * step, y, core], z_sent.at[way, step], z_got.at[way, step], target)
+
+    def z_sends(way, step):
+        return (above & (high >= step)) if way == 0 else (below & (high + step <= TALL - 1))
+
+    def z_comes(way, step):
+        return (high >= step + 1) if way == 0 else (high + step + 1 <= TALL - 1)
+
+    def z_step(step):
         for way in range(2):
-            if 0 < step <= steps[way]:
-                ring_wait(way, step - 1)
-            if step < steps[way]:
-                ring_copy(way, step).start()
+            if step > 0:
+
+                @pl.when(z_comes(way, step - 1))
+                def _():
+                    tile = land.at[high - (1 - 2 * way) * step, y, core]
+                    pltpu.make_async_copy(tile, tile, z_got.at[way, step - 1]).wait()
+
+            if step < TALL - 1:
+
+                @pl.when(z_sends(way, step))
+                def _():
+                    z_copy(way, step).start()
 
     def wide_copy(hop):
         target = at_owner(high, (y + hop) % WIDE, core)
@@ -218,15 +232,15 @@
     def router_step(step):
         if step == 0:
             line_wait()
-        if step <= steps[0]:
-            ring_step(step)
-        if step == steps[0]:
+        if step < TALL:
+            z_step(step)
+        if step == TALL - 1:
             for hop in range(1, WIDE):
                 wide_copy(hop).start()
-        if step == steps[0] + 1:
+        if step == TALL:
             wide_wait()
             core_copy().start()
-        if step == steps[0] + 2:
+        if step == TALL + 1:
             theirs = land.at[:, :, 1 - core]
             pltpu.make_async_copy(theirs, theirs, core_got.at[0]).wait()
             for first in range(0, TALL * WIDE * CORES, 16):
@@ -252,19 +266,23 @@
                 if slot - BEHIND < len(came):
                     source, (a, i) = came[slot - BEHIND]
                     arrived(source, a, i)
+        if slot % APART == APART // 2 and slot // APART <= TALL + 1:
+            router_step(slot // APART)
         for link in range(3):
             if slot < len(goes[link]):
                 source, (a, i) = goes[link][slot]
                 send(source, a, i, targets[link], link)
-        if slot % APART == APART // 2 and slot // APART <= steps[0] + 2:
-            router_step(slot // APART)
 
     for hop in range(1, 2 * SIDE):
         stat_copy(hop).wait_send()
         line_copy(hop).wait_send()
     for way in range(2):
-        for step in range(steps[way]):
-            ring_copy(way, step).wait_send()
+        for step in range(TALL - 1):
+
+            @pl.when(z_sends(way, step))
+            def _():
+                z_copy(way, step).wait_send()
+
     for hop in range(1, WIDE):
         wide_copy(hop).wait_send()
     core_copy().wait_send()
@@ -318,8 +336,8 @@
             pltpu.SemaphoreType.DMA((n, 32)),
             pltpu.SemaphoreType.DMA((n,)),
             pltpu.SemaphoreType.DMA((n,)),
-            pltpu.SemaphoreType.DMA((2, TALL // 2)),
-            pltpu.SemaphoreType.DMA((2, TALL // 2)),
+            pltpu.SemaphoreType.DMA((2, TALL - 1)),
+            pltpu.SemaphoreType.DMA((2, TALL - 1)),
             pltpu.SemaphoreType.DMA((WIDE,)),
             pltpu.SemaphoreType.DMA((WIDE,)),
             pltpu.SemaphoreType.DMA((1,)),

time: 77.5 us -> 76.2 us (0.983)
  the two profiles are of different devices: /device:TPU:1 before, /device:TPU:64 now
where the time goes in v4:
time: 76.2 us; the launch traced here: 76.1 us
  Pallas kernels  74.8 us (98%)
  between operations  1.29 us (2%)
    pallas_call x1, Pallas kernels, shards(): pl.pallas_call(gather_kernel, out_shape=(jax.ShapeDtypeStruct((2, n * sha...  71.4 us
    pallas_call x1, Pallas kernels, shards(): pl.pallas_call(place_kernel, out_shape=(jax.ShapeDtypeStruct((1, n * shar...  3.45 us

profile of v4, /device:TPU:64, one launch (start us, length us, event | category | flops | bytes accessed | tf_op | source)
XLA Modules:
  0.0 76.1 jit_solution(9034846621358826599)
XLA Ops:
  1.3 71.4 %gather.1 = (bf16[2,2048,1024]{2,1,0:T(8,128)(2,1)S(1)}, f32[2,1024]{1,0:T(2,128)S(1)}, bf16[64,2048]{1,0:T(8,128)(2,1)S(1)}) custom-call(f32[1]{0:T(128)S(6)} %copy.12.mix, f32[1,256,1024]{2,1,0:T(8,128)} %w_gate.1, f32[1,256,1024]{2,1,0:T(8,128)} %avg_gate.1, f32[1,256,1024]{2,1,0:T(8,128)} %w_up.1, f32[1,256,1024]{2,1,0:T(8,128)} %avg_up.1, ...), custom_call_target="tpu_custom_call" | custom-call | tf_op jit(solution)/shard_map/gather/pallas_call | solution.py:316
  72.7 3.4 %place.1 = (bf16[1,2048,1024]{2,1,0:T(8,128)(2,1)}, bf16[1,2048,1024]{2,1,0:T(8,128)(2,1)}, f32[1,1024]{1,0:T(1,128)}, f32[1,1024]{1,0:T(1,128)}, bf16[64,2048]{1,0:T(8,128)(2,1)}) custom-call(bf16[2,2048,1024]{2,1,0:T(8,128)(2,1)S(1)} %get-tuple-element.13.gathered, f32[2,1024]{1,0:T(2,128)S(1)} %get-tuple-element.14.scale, ...), custom_call_target="tpu_custom_call" | custom-call | tf_op jit(solution)/shard_map/place/pallas_call | solution.py:349

commit v5 on v4

--- a/solution.py
+++ b/solution.py
@@ -58,12 +58,12 @@
     for hop in range(1, 2 * SIDE):
         pl.semaphore_signal(barrier, inc=1, device_id={"rows": (me + hop) % (2 * SIDE)}, device_id_type=pl.DeviceIdType.MESH)
 
-    above, below = high < TALL - 1, high > 0
-    for there, step in ((above, 1), (below, -1)):
+    onward = 2 * z - 1
+    for there, step, row in ((high < TALL - 1, 1, x), (high > 0, -1, SIDE + x)):
 
         @pl.when(there)
         def _():
-            target = at_owner(high + step, y, core)
+            target = at_owner(high + step, y, core) | {"rows": row}
             pl.semaphore_signal(barrier, inc=1, device_id=target, device_id_type=pl.DeviceIdType.MESH)
 
     others = [at_owner(high, (y + hop) % WIDE, core) for hop in range(1, WIDE)]
@@ -90,7 +90,8 @@
     lanes = pl.ds(pl.multiple_of(me * share, share), share)
     land[high, y, core, :, lanes] = (line[0] * line[1]).astype(jnp.bfloat16).astype(jnp.float32)
 
-    greeted = 2 * SIDE - 1 + len(others) + above.astype(jnp.int32) + below.astype(jnp.int32)
+    has_next = (high + onward >= 0) & (high + onward < TALL)
+    greeted = 2 * SIDE - 1 + len(others) + 2 * has_next.astype(jnp.int32)
     pl.semaphore_wait(barrier, greeted)
 
     def stat_copy(hop):
@@ -119,31 +120,32 @@
     def line_copy(hop):
         return remote(line_place(me), line_sent.at[hop], line_got.at[me], {"rows": (me + hop) % (2 * SIDE)})
 
-    def z_copy(way, step):
-        towards = 1 - 2 * way
-        target = at_owner(high + towards, y, core)
-        return remote(land.at[high - towards * step, y, core], z_sent.at[way, step], z_got.at[way, step], target)
-
-    def z_sends(way, step):
-        return (above & (high >= step)) if way == 0 else (below & (high + step <= TALL - 1))
+    def z_copy(row, step):
+        target = at_owner(high + onward, y, core) | {"rows": (me, across)[row]}
+        return remote(land.at[high - onward * step, y, core], z_sent.at[row, step], z_got.at[1 - z, step], target)
+
+    def z_sends(step):
+        behind = high - onward * step
+        return has_next & (behind >= 0) & (behind < TALL)
 
     def z_comes(way, step):
         return (high >= step + 1) if way == 0 else (high + step + 1 <= TALL - 1)
 
     def z_step(step):
-        for way in range(2):
-            if step > 0:
+        if step > 0:
+            for way in range(2):
 
                 @pl.when(z_comes(way, step - 1))
                 def _():
                     tile = land.at[high - (1 - 2 * way) * step, y, core]
                     pltpu.make_async_copy(tile, tile, z_got.at[way, step - 1]).wait()
 
-            if step < TALL - 1:
-
-                @pl.when(z_sends(way, step))
-                def _():
-                    z_copy(way, step).start()
+        if step < TALL - 1:
+
+            @pl.when(z_sends(step))
+            def _():
+                for row in range(2):
+                    z_copy(row, step).start()
 
     def wide_copy(hop):
         target = at_owner(high, (y + hop) % WIDE, core)
@@ -276,12 +278,12 @@
     for hop in range(1, 2 * SIDE):
         stat_copy(hop).wait_send()
         line_copy(hop).wait_send()
-    for way in range(2):
-        for step in range(TALL - 1):
-
-            @pl.when(z_sends(way, step))
-            def _():
-                z_copy(way, step).wait_send()
+    for step in range(TALL - 1):
+
+        @pl.when(z_sends(step))
+        def _():
+            for row in range(2):
+                z_copy(row, step).wait_send()
 
     for hop in range(1, WIDE):
         wide_copy(hop).wait_send()

time: 76.2 us -> 74.9 us (0.983)
  the two profiles are of different devices: /device:TPU:64 before, /device:TPU:1 now
where the time goes in v5:
time: 74.9 us; the launch traced here: 73.8 us
  Pallas kernels  72.5 us (97%)
  between operations  1.29 us (2%)
    pallas_call x1, Pallas kernels, shards(): pl.pallas_call(gather_kernel, out_shape=(jax.ShapeDtypeStruct((2, n * sha...  69 us
    pallas_call x1, Pallas kernels, shards(): pl.pallas_call(place_kernel, out_shape=(jax.ShapeDtypeStruct((1, n * shar...  3.45 us

profile of v5, /device:TPU:1, one launch (start us, length us, event | category | flops | bytes accessed | tf_op | source)
XLA Modules:
  0.0 73.8 jit_solution(9080202655414433320)
XLA Ops:
  1.3 69.0 %gather.1 = (bf16[2,2048,1024]{2,1,0:T(8,128)(2,1)S(1)}, f32[2,1024]{1,0:T(2,128)S(1)}, bf16[64,2048]{1,0:T(8,128)(2,1)S(1)}) custom-call(f32[1]{0:T(128)S(6)} %copy.12.mix, f32[1,256,1024]{2,1,0:T(8,128)} %w_gate.1, f32[1,256,1024]{2,1,0:T(8,128)} %avg_gate.1, f32[1,256,1024]{2,1,0:T(8,128)} %w_up.1, f32[1,256,1024]{2,1,0:T(8,128)} %avg_up.1, ...), custom_call_target="tpu_custom_call" | custom-call | tf_op jit(solution)/shard_map/gather/pallas_call | solution.py:318
  70.3 3.4 %place.1 = (bf16[1,2048,1024]{2,1,0:T(8,128)(2,1)}, bf16[1,2048,1024]{2,1,0:T(8,128)(2,1)}, f32[1,1024]{1,0:T(1,128)}, f32[1,1024]{1,0:T(1,128)}, bf16[64,2048]{1,0:T(8,128)(2,1)}) custom-call(bf16[2,2048,1024]{2,1,0:T(8,128)(2,1)S(1)} %get-tuple-element.13.gathered, f32[2,1024]{1,0:T(2,128)S(1)} %get-tuple-element.14.scale, ...), custom_call_target="tpu_custom_call" | custom-call | tf_op jit(solution)/shard_map/place/pallas_call | solution.py:351

commit v6 on v5

--- a/solution.py
+++ b/solution.py
@@ -10,8 +10,9 @@
 SIDE = 4
 STEP = 16
 TALL, WIDE, CORES = 8, 4, 2
-BEHIND = 6
+BEHIND = 16
 APART = 7
+SPREAD = 172.0
 ACROSS = 9
 
 
@@ -23,7 +24,7 @@
 def gather_kernel(
     mix, w_gate, avg_gate, w_up, avg_up, weight, gain,
     out, scale, router,
-    fresh, other, stats, line, land, block,
+    coded, fresh, other, stats, factor, line, land, block,
     load, sent, stat_sent, stat_got, got,
     line_sent, line_got, z_sent, z_got, wide_sent, wide_got, core_sent, core_got,
 ):
@@ -158,16 +159,19 @@
         stat_copy(hop).start()
     for hop in range(1, 2 * SIDE):
         line_copy(hop).start()
-    for hop in range(1, 2 * SIDE):
-        source = (me + hop) % (2 * SIDE)
-        pltpu.make_async_copy(stats.at[source], stats.at[source], stat_got.at[source]).wait()
-    total = stats[0]
-    for source in range(1, 2 * SIDE):
-        total = total + stats[source]
-    scale[...] = jnp.sqrt(total)
+    def norms():
+        for hop in range(1, 2 * SIDE):
+            source = (me + hop) % (2 * SIDE)
+            pltpu.make_async_copy(stats.at[source], stats.at[source], stat_got.at[source]).wait()
+        total = stats[0]
+        for source in range(1, 2 * SIDE):
+            total = total + stats[source]
+        scale[...] = jnp.sqrt(total)
+        for source in range(2 * SIDE):
+            factor[source] = jnp.sqrt(stats[source]) / scale[...]
 
     def place(source, a, i):
-        return out.at[a, pl.ds(pl.multiple_of(source * share + i * STEP, STEP), STEP), :]
+        return coded.at[a, pl.ds(pl.multiple_of(source * share + i * STEP, STEP), STEP), :]
 
     def send(source, a, i, target, link):
         pltpu.make_async_remote_copy(
@@ -182,16 +186,37 @@
     def arrived(source, a, i):
         pltpu.make_async_copy(place(source, a, i), place(source, a, i), got.at[source, a * 16 + i]).wait()
 
-    def settle(a, i):
-        rows = pl.ds(pl.multiple_of(i * STEP, STEP), STEP)
-        value = fresh[a, rows, :] / scale[pl.ds(a, 1), :]
-        out[a, pl.ds(pl.multiple_of(me * share + i * STEP, STEP), STEP), :] = value.astype(jnp.bfloat16)
+    def rows_of(source, i):
+        return pl.ds(pl.multiple_of(source * share + i * STEP, STEP), STEP)
+
+    def own_norm(a):
+        total = stats[me, pl.ds(a, 1), :]
+        return jnp.where(total > 0.0, 1.0 / jnp.sqrt(total), 0.0)
+
+    over = (own_norm(0), own_norm(1))
+
+    def encode(a, i):
+        value = fresh[a, pl.ds(i * STEP, STEP), :]
+        size = jnp.exp(SPREAD * jnp.sqrt(jnp.abs(value) * over[a]) - 0.5 * SPREAD)
+        coded[a, rows_of(me, i), :] = jnp.where(value < 0.0, -size, size).astype(jnp.bfloat16)
+
+    def decode(source, a, i):
+        code = coded[a, rows_of(source, i), :].astype(jnp.float32)
+        root = jnp.log(jnp.abs(code)) * (1.0 / SPREAD) + 0.5
+        size = root * root * factor[source, pl.ds(a, 1), :]
+        out[a, rows_of(source, i), :] = jnp.where(code < 0.0, -size, size).astype(jnp.bfloat16)
+
+    def settle(k, _):
+        a, i = k // 16, k % 16
+        value = fresh[a, rows_of(0, i), :] / scale[pl.ds(a, 1), :]
+        out[a, rows_of(me, i), :] = value.astype(jnp.bfloat16)
+        return 0
 
     def flip(r):
         return (r + SIDE) % (2 * SIDE)
 
-    firsts = [chunk_at(k, True) for k in range(n_first)]
-    rests = [chunk_at(k, False) for k in range(n_rest)]
+    firsts = [(True, k) for k in range(n_first)]
+    rests = [(False, k) for k in range(n_rest)]
 
     def round_x(near, way):
         return (
@@ -205,19 +230,35 @@
 
     def from_x(near, way):
         return (
-            [(near, c) for c in rests]
-            + [(near, c) for c in firsts]
-            + [(far, c) for c in rests[way::2]]
-            + [(flip(near), c) for c in firsts]
-            + [(far, c) for c in firsts[way::2]]
-            + [(flip(far), c) for c in firsts[way::2]]
+            (near, rests),
+            (near, firsts),
+            (far, rests[way::2]),
+            (flip(near), firsts),
+            (far, firsts[way::2]),
+            (flip(far), firsts[way::2]),
         )
 
     def over_z(own, one, two, three):
-        return [(own, c) for c in firsts] + [(own, c) for c in rests] + [(r, c) for r in (one, two, three) for c in rests]
-
-    goes = (round_x(left, 0), round_x(right, 1), over_z(me, left, right, far))
-    comes = (from_x(left, 0), from_x(right, 1), over_z(across, flip(left), flip(right), flip(far)))
+        return ((own, firsts), (own, rests), (one, rests), (two, rests), (three, rests))
+
+    goes = (
+        round_x(left, 0),
+        round_x(right, 1),
+        [(source, c) for source, run in over_z(me, left, right, far) for c in run],
+    )
+    runs = (from_x(left, 0), from_x(right, 1), over_z(across, flip(left), flip(right), flip(far)))
+    comes = tuple([(source, run, at) for source, run in each for at in range(len(run))] for each in runs)
+
+    def decode_run(source, run, begin, end):
+        first, k = run[begin]
+        stride = run[1][1] - run[0][1]
+
+        def one(j, _):
+            decode(source, *chunk_at(k + stride * j, first))
+            return 0
+
+        lax.fori_loop(0, end - begin, one, 0)
+
     targets = (right, left, across)
     slots = max(len(g) for g in goes)
 
@@ -255,25 +296,36 @@
                 lax.fori_loop(0, 16, line_in, 0)
                 router[pl.ds(first, 16), :] = block[...].astype(jnp.bfloat16)
 
-    def settle_pair(k):
+    def encode_pair(k):
         for chunks in (firsts, rests):
             if k < len(chunks):
-                settle(*chunks[k])
-
-    settle_pair(0)
+                first, at = chunks[k]
+                encode(*chunk_at(at, first))
+
+    encode_pair(0)
+    waiting = [0, 0, 0]
     for slot in range(slots + BEHIND):
-        settle_pair(slot + 1)
-        if slot >= BEHIND:
-            for came in comes:
-                if slot - BEHIND < len(came):
-                    source, (a, i) = came[slot - BEHIND]
-                    arrived(source, a, i)
+        encode_pair(slot + 1)
+        if slot == BEHIND - 4:
+            norms()
+        if slot in range(BEHIND + 2, BEHIND + 18, 2):
+            at = (slot - BEHIND - 2) * 2
+            lax.fori_loop(at, at + 4, settle, 0)
+        for link in range(3):
+            at = slot - BEHIND
+            if 0 <= at < len(comes[link]):
+                source, run, j = comes[link][at]
+                arrived(source, *chunk_at(run[j][1], run[j][0]))
+                waiting[link] += 1
+                if waiting[link] == 6 or j == len(run) - 1 or at >= slots - 4:
+                    decode_run(source, run, j + 1 - waiting[link], j + 1)
+                    waiting[link] = 0
         if slot % APART == APART // 2 and slot // APART <= TALL + 1:
             router_step(slot // APART)
         for link in range(3):
             if slot < len(goes[link]):
-                source, (a, i) = goes[link][slot]
-                send(source, a, i, targets[link], link)
+                source, (first, at) = goes[link][slot]
+                send(source, *chunk_at(at, first), targets[link], link)
 
     for hop in range(1, 2 * SIDE):
         stat_copy(hop).wait_send()
@@ -290,7 +342,7 @@
     core_copy().wait_send()
     for link in range(3):
         count = len(goes[link])
-        all_sent = out.at[0, pl.ds(0, count * STEP), :]
+        all_sent = coded.at[0, pl.ds(0, count * STEP), :]
         pltpu.make_async_copy(all_sent, all_sent, sent.at[link]).wait()
 
 
@@ -325,8 +377,10 @@
         in_specs=[pl.BlockSpec(memory_space=pltpu.SMEM)] + [in_hbm] * 6,
         out_specs=(in_vmem,) * 3,
         scratch_shapes=[
+            pltpu.VMEM((2, n * share, width), jnp.bfloat16),
             pltpu.VMEM((2, share, width), jnp.float32),
             pltpu.VMEM((2, share, width), jnp.float32),
+            pltpu.VMEM((n, 2, width), jnp.float32),
             pltpu.VMEM((n, 2, width), jnp.float32),
             pltpu.VMEM((2, 1, share), jnp.float32),
             pltpu.VMEM((TALL, WIDE, CORES, 1, n * share), jnp.float32),

time: 74.9 us -> 71.2 us (0.951)
  Pallas kernels: 72.5 us -> 68.7 us
    pallas_call x1, Pallas kernels: 69 us -> 65.3 us  [shards(): pl.pallas_call(gather_kernel, out_shape=(jax.ShapeDtypeStruct((2, n * sha...]
where the time goes in v6:
time: 71.2 us; the launch traced here: 70 us
  Pallas kernels  68.7 us (96%)
  between operations  1.29 us (2%)
    pallas_call x1, Pallas kernels, shards(): pl.pallas_call(gather_kernel, out_shape=(jax.ShapeDtypeStruct((2, n * sha...  65.3 us
    pallas_call x1, Pallas kernels, shards(): pl.pallas_call(place_kernel, out_shape=(jax.ShapeDtypeStruct((1, n * shar...  3.45 us

profile of v6, /device:TPU:1, one launch (start us, length us, event | category | flops | bytes accessed | tf_op | source)
XLA Modules:
  0.0 70.0 jit_solution(10806943244851924083)
XLA Ops:
  1.3 65.3 %gather.1 = (bf16[2,2048,1024]{2,1,0:T(8,128)(2,1)S(1)}, f32[2,1024]{1,0:T(2,128)S(1)}, bf16[64,2048]{1,0:T(8,128)(2,1)S(1)}) custom-call(f32[1]{0:T(128)S(6)} %copy.12.mix, f32[1,256,1024]{2,1,0:T(8,128)} %w_gate.1, f32[1,256,1024]{2,1,0:T(8,128)} %avg_gate.1, f32[1,256,1024]{2,1,0:T(8,128)} %w_up.1, f32[1,256,1024]{2,1,0:T(8,128)} %avg_up.1, ...), custom_call_target="tpu_custom_call" | custom-call | tf_op jit(solution)/shard_map/gather/pallas_call | solution.py:370
  66.5 3.4 %place.1 = (bf16[1,2048,1024]{2,1,0:T(8,128)(2,1)}, bf16[1,2048,1024]{2,1,0:T(8,128)(2,1)}, f32[1,1024]{1,0:T(1,128)}, f32[1,1024]{1,0:T(1,128)}, bf16[64,2048]{1,0:T(8,128)(2,1)}) custom-call(bf16[2,2048,1024]{2,1,0:T(8,128)(2,1)S(1)} %get-tuple-element.13.gathered, f32[2,1024]{1,0:T(2,128)S(1)} %get-tuple-element.14.scale, ...), custom_call_target="tpu_custom_call" | custom-call | tf_op jit(solution)/shard_map/place/pallas_call | solution.py:405

commit v7 on v6

--- a/solution.py
+++ b/solution.py
@@ -12,6 +12,7 @@
 TALL, WIDE, CORES = 8, 4, 2
 BEHIND = 16
 APART = 7
+GROUP = 3
 SPREAD = 172.0
 ACROSS = 9
 
@@ -73,7 +74,8 @@
         pl.semaphore_signal(barrier, inc=1, device_id=target, device_id_type=pl.DeviceIdType.MESH)
 
     part = mix[0]
-    for a in range(2):
+
+    def sums(a):
         loads[2 * a].wait()
         loads[2 * a + 1].wait()
 
@@ -84,8 +86,11 @@
             return total + value * value
 
         total = lax.fori_loop(0, share // 8, mixed, jnp.zeros((8, fresh.shape[2]), jnp.float32), unroll=4)
-        stats[me, pl.ds(a, 1), :] = jnp.sum(total, axis=0, keepdims=True)
-
+        total = jnp.sum(total, axis=0, keepdims=True)
+        stats[me, pl.ds(a, 1), :] = total
+        return jnp.where(total > 0.0, 1.0 / jnp.sqrt(total), 0.0)
+
+    over = [sums(0)]
     loads[4].wait()
     loads[5].wait()
     lanes = pl.ds(pl.multiple_of(me * share, share), share)
@@ -99,8 +104,8 @@
         return pltpu.make_async_remote_copy(
             src_ref=stats.at[me],
             dst_ref=stats.at[me],
-            send_sem=stat_sent.at[hop],
-            recv_sem=stat_got.at[me],
+            send_sem=stat_sent.at[0],
+            recv_sem=stat_got.at[0],
             device_id={"rows": (me + hop) % (2 * SIDE)},
             device_id_type=pl.DeviceIdType.MESH,
         )
@@ -119,11 +124,11 @@
         return land.at[high, y, core, :, pl.ds(pl.multiple_of(source * share, share), share)]
 
     def line_copy(hop):
-        return remote(line_place(me), line_sent.at[hop], line_got.at[me], {"rows": (me + hop) % (2 * SIDE)})
+        return remote(line_place(me), line_sent.at[0], line_got.at[0], {"rows": (me + hop) % (2 * SIDE)})
 
     def z_copy(row, step):
         target = at_owner(high + onward, y, core) | {"rows": (me, across)[row]}
-        return remote(land.at[high - onward * step, y, core], z_sent.at[row, step], z_got.at[1 - z, step], target)
+        return remote(land.at[high - onward * step, y, core], z_sent.at[step], z_got.at[1 - z, step], target)
 
     def z_sends(step):
         behind = high - onward * step
@@ -150,19 +155,21 @@
 
     def wide_copy(hop):
         target = at_owner(high, (y + hop) % WIDE, core)
-        return remote(land.at[:, y, core], wide_sent.at[hop], wide_got.at[y], target)
+        return remote(land.at[:, y, core], wide_sent.at[0], wide_got.at[0], target)
 
     def core_copy():
         return remote(land.at[:, :, core], core_sent.at[0], core_got.at[0], at_owner(high, y, 1 - core))
 
-    for hop in range(1, 2 * SIDE):
-        stat_copy(hop).start()
+    def local_wait(place, sem):
+        pltpu.make_async_copy(place, place, sem).wait()
+
+    all_stats = stats.at[pl.ds(0, 2 * SIDE - 1)]
+    all_lines = land.at[0, 0, 0, :, pl.ds(0, (2 * SIDE - 1) * share)]
+    all_wide = land.at[:, pl.ds(0, WIDE - 1), 0]
     for hop in range(1, 2 * SIDE):
         line_copy(hop).start()
     def norms():
-        for hop in range(1, 2 * SIDE):
-            source = (me + hop) % (2 * SIDE)
-            pltpu.make_async_copy(stats.at[source], stats.at[source], stat_got.at[source]).wait()
+        local_wait(all_stats, stat_got.at[0])
         total = stats[0]
         for source in range(1, 2 * SIDE):
             total = total + stats[source]
@@ -173,27 +180,18 @@
     def place(source, a, i):
         return coded.at[a, pl.ds(pl.multiple_of(source * share + i * STEP, STEP), STEP), :]
 
-    def send(source, a, i, target, link):
+    def send(source, a, i, target, link, slot):
         pltpu.make_async_remote_copy(
             src_ref=place(source, a, i),
             dst_ref=place(source, a, i),
             send_sem=sent.at[link],
-            recv_sem=got.at[source, a * 16 + i],
+            recv_sem=got.at[link, slot // GROUP],
             device_id={"rows": target},
             device_id_type=pl.DeviceIdType.MESH,
         ).start()
 
-    def arrived(source, a, i):
-        pltpu.make_async_copy(place(source, a, i), place(source, a, i), got.at[source, a * 16 + i]).wait()
-
     def rows_of(source, i):
         return pl.ds(pl.multiple_of(source * share + i * STEP, STEP), STEP)
-
-    def own_norm(a):
-        total = stats[me, pl.ds(a, 1), :]
-        return jnp.where(total > 0.0, 1.0 / jnp.sqrt(total), 0.0)
-
-    over = (own_norm(0), own_norm(1))
 
     def encode(a, i):
         value = fresh[a, pl.ds(i * STEP, STEP), :]
@@ -263,14 +261,10 @@
     slots = max(len(g) for g in goes)
 
     def line_wait():
-        for hop in range(1, 2 * SIDE):
-            source = (me + hop) % (2 * SIDE)
-            pltpu.make_async_copy(line_place(source), line_place(source), line_got.at[source]).wait()
+        local_wait(all_lines, line_got.at[0])
 
     def wide_wait():
-        for hop in range(1, WIDE):
-            source = land.at[:, (y + hop) % WIDE, core]
-            pltpu.make_async_copy(source, source, wide_got.at[(y + hop) % WIDE]).wait()
+        local_wait(all_wide, wide_got.at[0])
 
     def router_step(step):
         if step == 0:
@@ -305,19 +299,25 @@
     encode_pair(0)
     waiting = [0, 0, 0]
     for slot in range(slots + BEHIND):
+        if slot == 3:
+            over.append(sums(1))
+            for hop in range(1, 2 * SIDE):
+                stat_copy(hop).start()
         encode_pair(slot + 1)
-        if slot == BEHIND - 4:
+        if slot == BEHIND - 1:
             norms()
-        if slot in range(BEHIND + 2, BEHIND + 18, 2):
-            at = (slot - BEHIND - 2) * 2
-            lax.fori_loop(at, at + 4, settle, 0)
+        if slot in range(BEHIND + 3, BEHIND + 19, 2):
+            begin = (slot - BEHIND - 3) * 2
+            lax.fori_loop(begin, begin + 4, settle, 0)
         for link in range(3):
             at = slot - BEHIND
-            if 0 <= at < len(comes[link]):
-                source, run, j = comes[link][at]
-                arrived(source, *chunk_at(run[j][1], run[j][0]))
+            if not 0 <= at < len(comes[link]) or (at % GROUP < GROUP - 1 and at < len(comes[link]) - 1):
+                continue
+            group = comes[link][at // GROUP * GROUP : at + 1]
+            local_wait(coded.at[0, pl.ds(0, len(group) * STEP), :], got.at[link, at // GROUP])
+            for source, run, j in group:
                 waiting[link] += 1
-                if waiting[link] == 6 or j == len(run) - 1 or at >= slots - 4:
+                if waiting[link] == 6 or j == len(run) - 1 or at >= slots - 6:
                     decode_run(source, run, j + 1 - waiting[link], j + 1)
                     waiting[link] = 0
         if slot % APART == APART // 2 and slot // APART <= TALL + 1:
@@ -325,20 +325,17 @@
         for link in range(3):
             if slot < len(goes[link]):
                 source, (first, at) = goes[link][slot]
-                send(source, *chunk_at(at, first), targets[link], link)
-
-    for hop in range(1, 2 * SIDE):
-        stat_copy(hop).wait_send()
-        line_copy(hop).wait_send()
+                send(source, *chunk_at(at, first), targets[link], link, slot)
+
+    local_wait(all_stats, stat_sent.at[0])
+    local_wait(all_lines, line_sent.at[0])
+    local_wait(all_wide, wide_sent.at[0])
     for step in range(TALL - 1):
 
         @pl.when(z_sends(step))
         def _():
-            for row in range(2):
-                z_copy(row, step).wait_send()
-
-    for hop in range(1, WIDE):
-        wide_copy(hop).wait_send()
+            local_wait(land.at[pl.ds(0, 2), 0, 0], z_sent.at[step])
+
     core_copy().wait_send()
     for link in range(3):
         count = len(goes[link])
@@ -347,13 +344,16 @@
 
 
 def place_kernel(gathered, scale, router, serve_gate, serve_up, scale_gate, scale_up, serve_router, done):
-    copies = (
-        pltpu.make_async_copy(gathered.at[pl.ds(0, 1)], serve_gate, done.at[0]),
-        pltpu.make_async_copy(gathered.at[pl.ds(1, 1)], serve_up, done.at[1]),
-        pltpu.make_async_copy(scale.at[pl.ds(0, 1)], scale_gate, done.at[2]),
-        pltpu.make_async_copy(scale.at[pl.ds(1, 1)], scale_up, done.at[3]),
-        pltpu.make_async_copy(router, serve_router, done.at[4]),
-    )
+    rows = gathered.shape[1] // 8
+    copies = [
+        pltpu.make_async_copy(scale.at[pl.ds(0, 1)], scale_gate, done.at[16]),
+        pltpu.make_async_copy(scale.at[pl.ds(1, 1)], scale_up, done.at[17]),
+        pltpu.make_async_copy(router, serve_router, done.at[18]),
+    ]
+    for a, target in enumerate((serve_gate, serve_up)):
+        for p in range(8):
+            piece = pl.ds(p * rows, rows)
+            copies.append(pltpu.make_async_copy(gathered.at[a, piece], target.at[0, piece], done.at[a * 8 + p]))
     for copy in copies:
         copy.start()
     for copy in copies:
@@ -387,15 +387,15 @@
             pltpu.VMEM((16, n * share), jnp.float32),
             pltpu.SemaphoreType.DMA((6,)),
             pltpu.SemaphoreType.DMA((3,)),
-            pltpu.SemaphoreType.DMA((n,)),
-            pltpu.SemaphoreType.DMA((n,)),
-            pltpu.SemaphoreType.DMA((n, 32)),
-            pltpu.SemaphoreType.DMA((n,)),
-            pltpu.SemaphoreType.DMA((n,)),
+            pltpu.SemaphoreType.DMA((1,)),
+            pltpu.SemaphoreType.DMA((1,)),
+            pltpu.SemaphoreType.DMA((3, 25)),
+            pltpu.SemaphoreType.DMA((1,)),
+            pltpu.SemaphoreType.DMA((1,)),
+            pltpu.SemaphoreType.DMA((TALL - 1,)),
             pltpu.SemaphoreType.DMA((2, TALL - 1)),
-            pltpu.SemaphoreType.DMA((2, TALL - 1)),
-            pltpu.SemaphoreType.DMA((WIDE,)),
-            pltpu.SemaphoreType.DMA((WIDE,)),
+            pltpu.SemaphoreType.DMA((1,)),
+            pltpu.SemaphoreType.DMA((1,)),
             pltpu.SemaphoreType.DMA((1,)),
             pltpu.SemaphoreType.DMA((1,)),
         ],
@@ -413,7 +413,7 @@
         ),
         in_specs=[in_vmem] * 3,
         out_specs=(in_hbm,) * 5,
-        scratch_shapes=[pltpu.SemaphoreType.DMA((5,))],
+        scratch_shapes=[pltpu.SemaphoreType.DMA((19,))],
         compiler_params=pltpu.CompilerParams(vmem_limit_bytes=32 * 2**20),
         name="place",
     )(gathered, scale, router)

time: 71.2 us -> 68.9 us (0.968); the launches traced: 70 us -> 68.5 us
  Pallas kernels: 68.7 us -> 67.2 us
    pallas_call x1, Pallas kernels: 65.3 us -> 63.6 us  [shards(): pl.pallas_call(gather_kernel, out_shape=(jax.ShapeDtypeStruct((2, n * sha...]
where the time goes in v7:
time: 68.9 us; the launch traced here: 68.5 us
  Pallas kernels  67.2 us (98%)
  between operations  1.29 us (2%)
    pallas_call x1, Pallas kernels, shards(): pl.pallas_call(gather_kernel, out_shape=(jax.ShapeDtypeStruct((2, n * sha...  63.6 us
    pallas_call x1, Pallas kernels, shards(): pl.pallas_call(place_kernel, out_shape=(jax.ShapeDtypeStruct((1, n * shar...  3.54 us

profile of v7, /device:TPU:1, one launch (start us, length us, event | category | flops | bytes accessed | tf_op | source)
XLA Modules:
  0.0 68.5 jit_solution(10299607856136881337)
XLA Ops:
  1.3 63.6 %gather.1 = (bf16[2,2048,1024]{2,1,0:T(8,128)(2,1)S(1)}, f32[2,1024]{1,0:T(2,128)S(1)}, bf16[64,2048]{1,0:T(8,128)(2,1)S(1)}) custom-call(f32[1]{0:T(128)S(6)} %copy.12.mix, f32[1,256,1024]{2,1,0:T(8,128)} %w_gate.1, f32[1,256,1024]{2,1,0:T(8,128)} %avg_gate.1, f32[1,256,1024]{2,1,0:T(8,128)} %w_up.1, f32[1,256,1024]{2,1,0:T(8,128)} %avg_up.1, ...), custom_call_target="tpu_custom_call" | custom-call | tf_op jit(solution)/shard_map/gather/pallas_call | solution.py:370
  64.9 3.5 %place.1 = (bf16[1,2048,1024]{2,1,0:T(8,128)(2,1)}, bf16[1,2048,1024]{2,1,0:T(8,128)(2,1)}, f32[1,1024]{1,0:T(1,128)}, f32[1,1024]{1,0:T(1,128)}, bf16[64,2048]{1,0:T(8,128)(2,1)}) custom-call(bf16[2,2048,1024]{2,1,0:T(8,128)(2,1)S(1)} %get-tuple-element.13.gathered, f32[2,1024]{1,0:T(2,128)S(1)} %get-tuple-element.14.scale, ...), custom_call_target="tpu_custom_call" | custom-call | tf_op jit(solution)/shard_map/place/pallas_call | solution.py:405

commit v8 on v7

--- a/solution.py
+++ b/solution.py
@@ -10,9 +10,9 @@
 SIDE = 4
 STEP = 16
 TALL, WIDE, CORES = 8, 4, 2
-BEHIND = 16
+BEHIND = 15
 APART = 7
-GROUP = 3
+GROUP = 4
 SPREAD = 172.0
 ACROSS = 9
 
@@ -54,7 +54,8 @@
         )
     ):
         loads.append(pltpu.make_async_copy(source, target, load.at[i]))
-        loads[-1].start()
+    for i in (0, 1, 4, 5):
+        loads[i].start()
 
     barrier = pltpu.get_barrier_semaphore()
     for hop in range(1, 2 * SIDE):
@@ -73,11 +74,14 @@
     for target in others:
         pl.semaphore_signal(barrier, inc=1, device_id=target, device_id_type=pl.DeviceIdType.MESH)
 
-    part = mix[0]
 
     def sums(a):
         loads[2 * a].wait()
         loads[2 * a + 1].wait()
+        if a == 0:
+            loads[2].start()
+            loads[3].start()
+        part = mix[0]
 
         def mixed(i, total):
             rows = pl.ds(pl.multiple_of(i * 8, 8), 8)
@@ -98,7 +102,6 @@
 
     has_next = (high + onward >= 0) & (high + onward < TALL)
     greeted = 2 * SIDE - 1 + len(others) + 2 * has_next.astype(jnp.int32)
-    pl.semaphore_wait(barrier, greeted)
 
     def stat_copy(hop):
         return pltpu.make_async_remote_copy(
@@ -166,8 +169,6 @@
     all_stats = stats.at[pl.ds(0, 2 * SIDE - 1)]
     all_lines = land.at[0, 0, 0, :, pl.ds(0, (2 * SIDE - 1) * share)]
     all_wide = land.at[:, pl.ds(0, WIDE - 1), 0]
-    for hop in range(1, 2 * SIDE):
-        line_copy(hop).start()
     def norms():
         local_wait(all_stats, stat_got.at[0])
         total = stats[0]
@@ -296,14 +297,18 @@
                 first, at = chunks[k]
                 encode(*chunk_at(at, first))
 
-    encode_pair(0)
+    for k in range(3):
+        encode_pair(k)
+    pl.semaphore_wait(barrier, greeted)
+    for hop in range(1, 2 * SIDE):
+        line_copy(hop).start()
     waiting = [0, 0, 0]
     for slot in range(slots + BEHIND):
         if slot == 3:
             over.append(sums(1))
             for hop in range(1, 2 * SIDE):
                 stat_copy(hop).start()
-        encode_pair(slot + 1)
+        encode_pair(slot + 3)
         if slot == BEHIND - 1:
             norms()
         if slot in range(BEHIND + 3, BEHIND + 19, 2):
@@ -320,8 +325,8 @@
                 if waiting[link] == 6 or j == len(run) - 1 or at >= slots - 6:
                     decode_run(source, run, j + 1 - waiting[link], j + 1)
                     waiting[link] = 0
-        if slot % APART == APART // 2 and slot // APART <= TALL + 1:
-            router_step(slot // APART)
+        if slot % APART == APART // 2 and 1 <= slot // APART <= TALL + 2:
+            router_step(slot // APART - 1)
         for link in range(3):
             if slot < len(goes[link]):
                 source, (first, at) = goes[link][slot]
@@ -344,16 +349,13 @@
 
 
 def place_kernel(gathered, scale, router, serve_gate, serve_up, scale_gate, scale_up, serve_router, done):
-    rows = gathered.shape[1] // 8
-    copies = [
-        pltpu.make_async_copy(scale.at[pl.ds(0, 1)], scale_gate, done.at[16]),
-        pltpu.make_async_copy(scale.at[pl.ds(1, 1)], scale_up, done.at[17]),
-        pltpu.make_async_copy(router, serve_router, done.at[18]),
-    ]
-    for a, target in enumerate((serve_gate, serve_up)):
-        for p in range(8):
-            piece = pl.ds(p * rows, rows)
-            copies.append(pltpu.make_async_copy(gathered.at[a, piece], target.at[0, piece], done.at[a * 8 + p]))
+    copies = (
+        pltpu.make_async_copy(gathered.at[pl.ds(0, 1)], serve_gate, done.at[0]),
+        pltpu.make_async_copy(gathered.at[pl.ds(1, 1)], serve_up, done.at[1]),
+        pltpu.make_async_copy(scale.at[pl.ds(0, 1)], scale_gate, done.at[2]),
+        pltpu.make_async_copy(scale.at[pl.ds(1, 1)], scale_up, done.at[3]),
+        pltpu.make_async_copy(router, serve_router, done.at[4]),
+    )
     for copy in copies:
         copy.start()
     for copy in copies:
@@ -389,7 +391,7 @@
             pltpu.SemaphoreType.DMA((3,)),
             pltpu.SemaphoreType.DMA((1,)),
             pltpu.SemaphoreType.DMA((1,)),
-            pltpu.SemaphoreType.DMA((3, 25)),
+            pltpu.SemaphoreType.DMA((3, 19)),
             pltpu.SemaphoreType.DMA((1,)),
             pltpu.SemaphoreType.DMA((1,)),
             pltpu.SemaphoreType.DMA((TALL - 1,)),
@@ -413,7 +415,7 @@
         ),
         in_specs=[in_vmem] * 3,
         out_specs=(in_hbm,) * 5,
-        scratch_shapes=[pltpu.SemaphoreType.DMA((19,))],
+        scratch_shapes=[pltpu.SemaphoreType.DMA((5,))],
         compiler_params=pltpu.CompilerParams(vmem_limit_bytes=32 * 2**20),
         name="place",
     )(gathered, scale, router)

time: 68.9 us -> 67.7 us (0.983)
  the two profiles are of different devices: /device:TPU:1 before, /device:TPU:120 now
where the time goes in v8:
time: 67.7 us; the launch traced here: 67.5 us
  Pallas kernels  66.3 us (98%)
  between operations  1.29 us (2%)
    pallas_call x1, Pallas kernels, shards(): pl.pallas_call(gather_kernel, out_shape=(jax.ShapeDtypeStruct((2, n * sha...  62.8 us
    pallas_call x1, Pallas kernels, shards(): pl.pallas_call(place_kernel, out_shape=(jax.ShapeDtypeStruct((1, n * shar...  3.45 us

profile of v8, /device:TPU:120, one launch (start us, length us, event | category | flops | bytes accessed | tf_op | source)
XLA Modules:
  0.0 67.5 jit_solution(9278549872681341044)
XLA Ops:
  1.3 62.8 %gather.1 = (bf16[2,2048,1024]{2,1,0:T(8,128)(2,1)S(1)}, f32[2,1024]{1,0:T(2,128)S(1)}, bf16[64,2048]{1,0:T(8,128)(2,1)S(1)}) custom-call(f32[1]{0:T(128)S(6)} %copy.12.mix, f32[1,256,1024]{2,1,0:T(8,128)} %w_gate.1, f32[1,256,1024]{2,1,0:T(8,128)} %avg_gate.1, f32[1,256,1024]{2,1,0:T(8,128)} %w_up.1, f32[1,256,1024]{2,1,0:T(8,128)} %avg_up.1, ...), custom_call_target="tpu_custom_call" | custom-call | tf_op jit(solution)/shard_map/gather/pallas_call | solution.py:372
  64.1 3.4 %place.1 = (bf16[1,2048,1024]{2,1,0:T(8,128)(2,1)}, bf16[1,2048,1024]{2,1,0:T(8,128)(2,1)}, f32[1,1024]{1,0:T(1,128)}, f32[1,1024]{1,0:T(1,128)}, bf16[64,2048]{1,0:T(8,128)(2,1)}) custom-call(bf16[2,2048,1024]{2,1,0:T(8,128)(2,1)S(1)} %get-tuple-element.13.gathered, f32[2,1024]{1,0:T(2,128)S(1)} %get-tuple-element.14.scale, ...), custom_call_target="tpu_custom_call" | custom-call | tf_op jit(solution)/shard_map/place/pallas_call | solution.py:407

commit v9 on v8

--- a/solution.py
+++ b/solution.py
@@ -27,7 +27,7 @@
     out, scale, router,
     coded, fresh, other, stats, factor, line, land, block,
     load, sent, stat_sent, stat_got, got,
-    line_sent, line_got, z_sent, z_got, wide_sent, wide_got, core_sent, core_got,
+    line_sent, line_got, z_sent, z_got, wide_sent, wide_got, core_sent, core_got, above_in,
 ):
     me = lax.axis_index("rows")
     owner = lax.axis_index("owner")
@@ -62,12 +62,11 @@
         pl.semaphore_signal(barrier, inc=1, device_id={"rows": (me + hop) % (2 * SIDE)}, device_id_type=pl.DeviceIdType.MESH)
 
     onward = 2 * z - 1
-    for there, step, row in ((high < TALL - 1, 1, x), (high > 0, -1, SIDE + x)):
-
-        @pl.when(there)
-        def _():
-            target = at_owner(high + step, y, core) | {"rows": row}
-            pl.semaphore_signal(barrier, inc=1, device_id=target, device_id_type=pl.DeviceIdType.MESH)
+
+    @pl.when(high < TALL - 1)
+    def _():
+        target = at_owner(high + 1, y, core) | {"rows": x}
+        pl.semaphore_signal(barrier, inc=1, device_id=target, device_id_type=pl.DeviceIdType.MESH)
 
     others = [at_owner(high, (y + hop) % WIDE, core) for hop in range(1, WIDE)]
     others.append(at_owner(high, y, 1 - core))
@@ -101,7 +100,8 @@
     land[high, y, core, :, lanes] = (line[0] * line[1]).astype(jnp.bfloat16).astype(jnp.float32)
 
     has_next = (high + onward >= 0) & (high + onward < TALL)
-    greeted = 2 * SIDE - 1 + len(others) + 2 * has_next.astype(jnp.int32)
+    sends_down, sends_up = (z == 0) & (high > 0), (z == 1) & (high < TALL - 1)
+    greeted = 2 * SIDE - 1 + len(others) + 2 * sends_down.astype(jnp.int32)
 
     def stat_copy(hop):
         return pltpu.make_async_remote_copy(
@@ -270,6 +270,11 @@
     def router_step(step):
         if step == 0:
             line_wait()
+
+            @pl.when(sends_up)
+            def _():
+                pl.semaphore_wait(above_in, 1)
+
         if step < TALL:
             z_step(step)
         if step == TALL - 1:
@@ -300,6 +305,12 @@
     for k in range(3):
         encode_pair(k)
     pl.semaphore_wait(barrier, greeted)
+
+    @pl.when(sends_down)
+    def _():
+        target = at_owner(high - 1, y, core) | {"rows": SIDE + x}
+        pl.semaphore_signal(above_in, inc=1, device_id=target, device_id_type=pl.DeviceIdType.MESH)
+
     for hop in range(1, 2 * SIDE):
         line_copy(hop).start()
     waiting = [0, 0, 0]
@@ -400,6 +411,7 @@
             pltpu.SemaphoreType.DMA((1,)),
             pltpu.SemaphoreType.DMA((1,)),
             pltpu.SemaphoreType.DMA((1,)),
+            pltpu.SemaphoreType.REGULAR,
         ],
         compiler_params=pltpu.CompilerParams(collective_id=0, has_side_effects=True, vmem_limit_bytes=32 * 2**20),
         name="gather",

time: 67.7 us -> 67.4 us (level)
  the two profiles are of different devices: /device:TPU:120 before, /device:TPU:2 now
where the time goes in v9:
time: 67.4 us; the launch traced here: 67.2 us
  Pallas kernels  65.9 us (98%)
  between operations  1.29 us (2%)
    pallas_call x1, Pallas kernels, shards(): pl.pallas_call(gather_kernel, out_shape=(jax.ShapeDtypeStruct((2, n * sha...  62.5 us
    pallas_call x1, Pallas kernels, shards(): pl.pallas_call(place_kernel, out_shape=(jax.ShapeDtypeStruct((1, n * shar...  3.45 us

profile of v9, /device:TPU:2, one launch (start us, length us, event | category | flops | bytes accessed | tf_op | source)
XLA Modules:
  0.0 67.2 jit_solution(9187925745676350857)
XLA Ops:
  1.3 62.5 %gather.1 = (bf16[2,2048,1024]{2,1,0:T(8,128)(2,1)S(1)}, f32[2,1024]{1,0:T(2,128)S(1)}, bf16[64,2048]{1,0:T(8,128)(2,1)S(1)}) custom-call(f32[1]{0:T(128)S(6)} %copy.12.mix, f32[1,256,1024]{2,1,0:T(8,128)} %w_gate.1, f32[1,256,1024]{2,1,0:T(8,128)} %avg_gate.1, f32[1,256,1024]{2,1,0:T(8,128)} %w_up.1, f32[1,256,1024]{2,1,0:T(8,128)} %avg_up.1, ...), custom_call_target="tpu_custom_call" | custom-call | tf_op jit(solution)/shard_map/gather/pallas_call | solution.py:383
  63.7 3.4 %place.1 = (bf16[1,2048,1024]{2,1,0:T(8,128)(2,1)}, bf16[1,2048,1024]{2,1,0:T(8,128)(2,1)}, f32[1,1024]{1,0:T(1,128)}, f32[1,1024]{1,0:T(1,128)}, bf16[64,2048]{1,0:T(8,128)(2,1)}) custom-call(bf16[2,2048,1024]{2,1,0:T(8,128)(2,1)S(1)} %get-tuple-element.13.gathered, f32[2,1024]{1,0:T(2,128)S(1)} %get-tuple-element.14.scale, ...), custom_call_target="tpu_custom_call" | custom-call | tf_op jit(solution)/shard_map/place/pallas_call | solution.py:419
